TPU v7x, 256 devices: a whole 4x4x8 slice. The times are simulated.
256 devices in a mesh: band: 64 (over z, y_hi, x), ga: 4 (over y_lo, core).
Axes of the slice: x: 4, y: 4 (y_hi: 2, y_lo: 2; y = y_hi * 2 + y_lo), z: 8, core: 2. Of those that a mesh axis runs over, the one named last changes fastest.
Arguments:
- elements: bfloat16 [2, 6144, 2048], P(None, 'band', 'ga'), may hold values from -0.75 to 0.75
- screened: bfloat16 [2, 2, 2048, 2048], P(None, None, 'ga'), may hold values from -0.09375 to 0.09375
- energies: float32 [6144], replicated, may hold values from -3 to 3
- freq_points: float32 [2], replicated, may hold values from -3 to 3
- freq_weights: float32 [2], replicated, may hold values from 0.5 to 2
- band_of_slot: int32 [6144], replicated, may hold values from 0 to 6143, each once
Outputs:
- sigma: float32 [2, 6144, 6144], P(None, 'band', 'ga')
Inputs may be any that keep to these rules, and one draw needn't show every extreme that they name: `band_of_slot`: each of 0 to 6143 stands once.
All inputs are finite; a program needn't handle non-finite values.
Results may differ from a plain program's by a relative error of at most 0.0042.
Values may be sent and summed in bfloat16 or wider, within the bound.
A program may use at most 128 MiB of HBM per device.

v0:
```python
import jax
import jax.numpy as jnp
from jax import lax
from jax.sharding import Mesh
from jax.sharding import PartitionSpec as P

GA = ("ga_0", "ga_1")


def in_order(blocks, dim):
    shape = list(blocks.shape[1:])
    shape[dim] *= blocks.shape[0]
    return jnp.moveaxis(blocks, 0, dim).reshape(shape)


def all_blocks(shard, axes, order):
    blocks = shard
    for k in order:
        blocks = lax.all_gather(blocks, axes[k])
    done = order[::-1]
    back = [done.index(k) for k in range(len(axes))]
    blocks = blocks.transpose(*back, *range(len(axes), blocks.ndim))
    return blocks.reshape(-1, *shard.shape)


def gathered_by_axis(shard, axes, order, dim):
    return in_order(all_blocks(shard, axes, order), dim)


def split_up(shard, dim, peers):
    shape = shard.shape
    blocks = shard.reshape(*shape[:dim], peers, shape[dim] // peers, *shape[dim + 1 :])
    return jnp.moveaxis(blocks, dim, 0)


def summed_on_arrival(shard, axis, dim):
    blocks = split_up(shard, dim, lax.axis_size(axis))
    arrived = lax.all_to_all(blocks, axis, split_axis=0, concat_axis=0, tiled=True)
    return arrived.astype(jnp.float32).sum(axis=0)


def make_left(block):
    flipped = jnp.stack([-block[1], block[0]])
    return jnp.stack([block, flipped])


def on_device(elements, screened, energies, freq_points, freq_weights, band_of_slot):
    bands = elements.shape[1]
    slot_energy = jnp.take(energies, band_of_slot)
    offset = slot_energy[None, :] - freq_points[:, None]
    screen = freq_weights[:, None] / (1.0 + 4.0 * offset * offset)
    own_start = lax.axis_index("band") * bands
    screen_own = lax.dynamic_slice_in_dim(screen, own_start, bands, 1)
    piece = gathered_by_axis(elements, GA, (0, 1), 2)
    real_side = jnp.stack([piece[0], -piece[1]])
    imag_side = jnp.stack([piece[1], piece[0]])
    sides = jnp.stack([real_side, imag_side])
    applied = jnp.einsum(
        "dcmk,wcgk->wdmg", sides, screened, preferred_element_type=jnp.float32
    ).astype(jnp.bfloat16)
    left_own = make_left(elements)
    pairs = jnp.einsum(
        "dcnk,wcmk->wdnm",
        left_own,
        lax.all_gather(applied, "band", axis=2, tiled=True),
        preferred_element_type=jnp.float32,
    )
    factor = 0.5 * (screen_own[:, :, None] + screen[:, None, :])
    partial_rows = jnp.sum(pairs * factor[:, None], axis=0)
    return summed_on_arrival(partial_rows.astype(jnp.bfloat16), GA, 2)


def solution(mesh):
    torus = Mesh(mesh.devices.reshape(mesh.shape["band"], 2, 2), ("band", "ga_0", "ga_1"))
    return jax.shard_map(
        on_device,
        mesh=torus,
        in_specs=(P(None, "band", GA), P(None, None, GA, None), P(), P(), P(), P()),
        out_specs=P(None, "band", GA),
        check_vma=False,
    )
```

profile of v0, /device:TPU:1, one launch (start us, length us, event | category | flops | bytes accessed | tf_op | source)
XLA Modules:
  0.0 343.5 jit_solution(7880529084560656010)
XLA Ops:
  6.5 0.0 copy-start
  6.5 0.0 all-gather.4.cloned.1.call-start
  6.5 6.5 %all-gather = bf16[4,96,512]{2,1,0:T(8,128)(2,1)S(1)} all-gather(bf16[2,96,512]{2,1,0:T(8,128)(2,1)} %param.6), channel_id=2, replica_groups=mesh['band'=64,'ga_0'=2,'ga_1'=2] {'ga_0'}, dimensions={0}, use_global_device_ids=true | all-gather | bytes 589824 | tf_op jit(solution)/shard_map/all_gather | solution.py:19
  13.0 0.0 copy-start.5
  13.0 5.5 %all-gather.1 = bf16[4,2,96,512]{3,2,1,0:T(8,128)(2,1)S(1)} all-gather(bf16[2,2,96,512]{3,2,1,0:T(8,128)(2,1)S(1)} %bitcast.72), channel_id=3, replica_groups=mesh['band'=64,'ga_0'=2,'ga_1'=2] {'ga_1'}, dimensions={0}, use_global_device_ids=true | all-gather | bytes 1179648 | tf_op jit(solution)/shard_map/all_gather | solution.py:19
  18.5 0.1 copy.15
  18.6 0.1 slice_bitcast_fusion
  18.7 0.1 neg.14
  18.8 0.1 maximum_bitcast_fusion.8
  18.9 0.0 copy-done.5
  19.0 0.0 copy-start.2
  19.0 3.7 %fusion.15 = bf16[2,2,96,512]{3,2,1,0:T(8,128)(2,1)} fusion(bf16[2,2,512,2048]{3,2,1,0:T(8,128)(2,1)S(1)} %copy-done.5, bf16[1,2,96,2048]{3,2,1,0:T(8,128)(2,1)S(1)} %get-tuple-element.8, bf16[1,2,96,2048]{3,2,1,0:T(8,128)(2,1)S(1)} %get-tuple-element.7), kind=kOutput, calls=%fused_computation.14 | convolution fusion | flops 1613955072 | bytes 10354688 | tf_op jit(solution)/shard_map/dcmk,wcgk->wdmg/dot_general | solution.py:58
  22.6 0.0 all-gather.4.cloned.1.call-update
  22.7 0.0 copy-done.2
  22.7 0.0 copy-done
  22.7 0.0 copy-start.3
  22.7 0.0 copy-start.4
  22.7 0.0 copy-start.1
  22.7 34.3 %gather_fusion = f32[6144]{0:T(1024)S(1)} fusion(f32[6144]{0:T(1024)S(1)} %copy-done, s32[6144]{0:T(1024)S(1)} %fusion.22), kind=kCustom, calls=%fused_computation | custom fusion | bytes 73728 | tf_op jit(solution)/shard_map/jit(_take)/gather | solution.py:49
  57.0 0.0 copy-done.3
  57.1 0.0 copy-done.4
  57.1 0.1 fusion.21
  57.2 0.1 constant_dynamic-slice_fusion
  57.3 0.0 copy-done.1
  57.3 2.7 add_multiply_fusion
  60.0 223.9 %all-gather.4.cloned.1.call-done = bf16[2,2,6144,512]{3,2,1,0:T(8,128)(2,1)} async-done(((bf16[2,2,96,512]{3,2,1,0:T(8,128)(2,1)}), bf16[2,2,6144,512]{3,2,1,0:T(8,128)(2,1)}) %all-gather.4.cloned.1.call-update) | async-done | bytes 25165840 | tf_op jit(solution)/shard_map/all_gather | solution.py:65
  284.0 16.0 %fusion.2 = bf16[2,96,6144]{2,1,0:T(8,128)(2,1)} fusion(bf16[2,2,6144,512]{3,2,1,0:T(8,128)(2,1)} %all-gather.4.cloned.1.call-done, f32[2,96,6144]{2,1,0:T(8,128)} %add_multiply_fusion, bf16[1,2,96,512]{3,2,1,0:T(8,128)(2,1)S(1)} %maximum_bitcast_fusion.12, bf16[1,2,96,512]{3,2,1,0:T(8,128)(2,1)S(1)} %bitcast.74), kind=kOutput, calls=%fused_computation.4 | convolution fusion | flops 4836163584 | bytes 32636928 | tf_op jit(solution)/shard_map/dcnk,wcmk->wdnm/dot_general | solution.py:62
  300.0 3.5 %convert_element_type.19 = bf16[2,96,4,1536]{3,2,1,0:T(4,128)(2,1)S(1)} reshape(bf16[2,96,6144]{2,1,0:T(8,128)(2,1)} %fusion.2) | data formatting | bytes 4718592 | tf_op jit(solution)/shard_map/convert_element_type | solution.py:70
  303.5 0.4 copy.18
  303.9 31.3 %all_to_all.5 = bf16[4,2,96,1536]{3,2,1,0:T(8,128)(2,1)S(1)} all-to-all(bf16[4,2,96,1536]{3,2,1,0:T(8,128)(2,1)S(1)} %copy.18), channel_id=1, replica_groups=mesh['band'=64,'ga_0'=2,'ga_1'=2] {'ga_0','ga_1'}, dimensions={0} | all-to-all | bytes 4718592 | tf_op jit(solution)/shard_map/all_to_all | solution.py:38
  335.2 1.4 convert_reduce_fusion
  (6 shorter events, 0.1 us)
Async XLA Ops:
  6.5 16.2 %copy-start = (f32[6144]{0:T(1024)S(1)}, f32[6144]{0:T(1024)}, u32[]{:S(2)}) copy-start(f32[6144]{0:T(1024)} %param.8) | copy-start | bytes 73732
  6.5 277.5 %all-gather.4.cloned.1.call-start = ((), (), s32[]{:S(2)}) async-start(), calls=%async_computation.1 | async-start | bytes 25559040 | tf_op jit(solution)/shard_map/all_gather | solution.py:65
  13.0 5.9 %copy-start.5 = (bf16[2,2,512,2048]{3,2,1,0:T(8,128)(2,1)S(1)}, bf16[2,2,512,2048]{3,2,1,0:T(8,128)(2,1)}, u32[]{:S(2)}) copy-start(bf16[2,2,512,2048]{3,2,1,0:T(8,128)(2,1)} %param.7) | copy-start | bytes 25165828
  19.0 3.7 %copy-start.2 = (s32[6144]{0:T(1024)S(1)}, s32[6144]{0:T(1024)}, u32[]{:S(2)}) copy-start(s32[6144]{0:T(1024)} %param.11) | copy-start | bytes 73732
  22.7 34.3 %copy-start.3 = (f32[2]{0:T(128)S(1)}, f32[2]{0:T(128)}, u32[]{:S(2)}) copy-start(f32[2]{0:T(128)} %param.10) | copy-start | bytes 28
  22.7 34.3 %copy-start.4 = (f32[2]{0:T(128)S(1)}, f32[2]{0:T(128)}, u32[]{:S(2)}) copy-start(f32[2]{0:T(128)} %param.9) | copy-start | bytes 28
  22.7 34.5 %copy-start.1 = (bf16[2,96,512]{2,1,0:T(8,128)(2,1)S(1)}, bf16[2,96,512]{2,1,0:T(8,128)(2,1)}, u32[]{:S(2)}) copy-start(bf16[2,96,512]{2,1,0:T(8,128)(2,1)} %param.6) | copy-start | bytes 589828
Sparse Core Ops, SparseCore 0:
  22.8 261.1 all-gather.3
where the time goes:
time: 344 us; the launch traced here: 343 us
  waiting for transfers between devices  224 us (65%)
  blocking collectives  43.3 us (13%)
  local copies, waits for them, and re-layouts  38.5 us (11%)
  matrix products  19.6 us (6%)
  between operations  13.6 us (4%)
  other arithmetic  4.5 us (1%)
    all_gather x1, waiting for transfers between devices, on_device(): lax.all_gather(applied, 'band', axis=2, tiled=True)  224 us
    gather x1, local copies, waits for them, and re-layouts, on_device(): slot_energy = jnp.take(energies, band_of_slot)  34.3 us
    all_to_all x1, blocking collectives, summed_on_arrival(): lax.all_to_all(blocks, axis, split_axis=0, concat_axis=0, tiled=True)  31.3 us
    dot_general x1, matrix products, on_device(): jnp.einsum('dcnk,wcmk->wdnm', left_own, lax.all_gather(applied, 'band', a...  16 us
    all_gather x2, blocking collectives, all_blocks(): blocks = lax.all_gather(blocks, axes[k])  12 us
  transfers between devices with their start and end apart: 1, of which 1 were waited for; matrix products, arithmetic and copies ran while one was open for 11% of the time, Pallas kernels for 0%

commit v1 on v0

v1 whole, which is shorter than its diff:
```python
import jax
import jax.numpy as jnp
from jax import lax
from jax.experimental import pallas as pl
from jax.experimental.pallas import tpu as pltpu
from jax.sharding import Mesh
from jax.sharding import PartitionSpec as P

BAND = ("z", "yh", "x")
GA = ("yl", "c")
F32 = jnp.float32
BF16 = jnp.bfloat16


def dot_t(a, b):
    return lax.dot_general(a, b, (((1,), (1,)), ((), ())), preferred_element_type=F32)


def kernel(
    elements, screened, energies, bands, points, weights, out,
    e_full, e_plane, w_buf, acc, y_buf, y_swap, s_sum, x_send, x_recv, o_buf, o_recv, s_col, s_row,
    load_sem, p_send, p_recv, a_send, a_recv, xr_send, xr_recv, z_send, z_recv,
    d_send, d_recv, o_send, o_sem,
):
    z, yh, x, yl, c = (lax.axis_index(name) for name in ("z", "yh", "x", "yl", "c"))
    own_q = yl * 2 + c
    own_b = yh * 4 + x
    slots = e_full.shape[2]

    def remote(src, dst, send, recv, **device):
        return pltpu.make_async_remote_copy(
            src_ref=src, dst_ref=dst, send_sem=send, recv_sem=recv,
            device_id=device, device_id_type=pl.DeviceIdType.MESH)

    quarter = [own_q, yl * 2 + (1 - c), (1 - yl) * 2 + c, (1 - yl) * 2 + (1 - c)]
    load_e = pltpu.make_async_copy(elements, e_full.at[own_q], load_sem.at[0])
    load_p = pltpu.make_async_copy(elements, e_plane.at[:, own_b], load_sem.at[1])
    load_e.start()
    load_p.start()
    load_w = []
    for k in range(4):
        at = pl.multiple_of(quarter[k] * 512, 512)
        load_w.append(pltpu.make_async_copy(screened.at[:, :, :, pl.ds(at, 512)], w_buf.at[k], load_sem.at[2 + k]))
        load_w[k].start()

    barrier = pltpu.get_barrier_semaphore()

    def greet(**device):
        pl.semaphore_signal(barrier, inc=1, device_id=device, device_id_type=pl.DeviceIdType.MESH)

    def plane(dyh, dx, dyl):
        return dict(yh=lax.rem(yh + dyh, 2), x=lax.rem(x + dx, 4), yl=lax.rem(yl + dyl, 2))

    greet(c=1 - c)
    z_up, z_down = lax.rem(z + 1, 8), lax.rem(z + 7, 8)
    greet(z=z_up)
    greet(z=z_down)
    for dyh in range(2):
        for dx in range(4):
            for dyl in range(2):
                if dyh or dx or dyl:
                    greet(**plane(dyh, dx, dyl))
    pl.semaphore_wait(barrier, 18)
    load_e.wait()

    to_y = remote(e_full.at[own_q], e_full.at[own_q], p_send.at[0], p_recv.at[0], yl=1 - yl)
    to_c = remote(e_full.at[own_q], e_full.at[own_q], p_send.at[1], p_recv.at[1], c=1 - c)
    to_y.start()
    to_c.start()
    load_p.wait()

    x_up, x_down = lax.rem(x + 1, 4), lax.rem(x + 3, 4)

    def block_at(k, at_x):
        return (yh if k == 0 else 1 - yh) * 4 + at_x

    def x_copy(k, way, hop):
        ahead, behind = (x_up, x_down) if way == 0 else (x_down, x_up)
        if hop == 1:
            ref = e_plane.at[:, block_at(k, x)]
        else:
            ref = e_plane.at[way, block_at(k, behind)]
        return remote(ref, ref, xr_send.at[k, way, hop - 1], xr_recv.at[k, way, hop - 1], x=ahead)

    for way in range(2):
        x_copy(0, way, 1).start()

    def accumulate(k, first):
        lhs = e_full[quarter[k]].reshape(2 * slots, 512)

        def one(i, carry):
            term = dot_t(lhs, w_buf[k, i // 2, i % 2])
            acc[i] = term if first else acc[i] + term
            return carry

        lax.fori_loop(0, 4, one, 0)

    load_w[0].wait()
    accumulate(0, True)

    def look_up(i, carry):
        at = jnp.where(i < 8, z * 8 + i, (i - 8) * 8 + own_b)
        band = jnp.broadcast_to(bands[pl.ds(at, 1), :], (128, slots)).T
        lane = lax.broadcasted_iota(jnp.int32, (slots, 128), 1)

        def part(j, total):
            for u in range(4):
                row = j * 4 + u
                e = jnp.broadcast_to(energies[pl.ds(row, 1), :], (slots, 128))
                total = total + jnp.where(band == lane + row * 128, e, 0.0)
            return total

        total = lax.fori_loop(0, 12, part, jnp.zeros((slots, 128), F32))
        energy = jnp.broadcast_to(jnp.sum(total, axis=1, keepdims=True), (slots, 128))
        for w in range(2):
            offset = energy - points[w]
            s_col[w, i] = weights[w] / (1.0 + 4.0 * offset * offset)
        return carry

    lax.fori_loop(0, 16, look_up, 0)

    def turn(i, carry):
        w, g = i // 4, i % 4
        one, two = s_col[w, 8 + 2 * g], s_col[w, 9 + 2 * g]
        s_row[w, g] = jnp.concatenate([one, one, two, two], axis=0).T[0:8]
        return carry

    lax.fori_loop(0, 8, turn, 0)

    to_c.wait_recv()
    load_w[1].wait()
    accumulate(1, False)

    to_y.wait_recv()
    other = e_full.at[quarter[2]]
    pass_c = remote(other, other, p_send.at[2], p_recv.at[2], c=1 - c)
    pass_c.start()
    to_a = remote(other, e_plane.at[:, own_b], a_send, a_recv, yh=1 - yh, yl=1 - yl)
    to_a.start()
    load_w[2].wait()
    accumulate(2, False)
    load_w[3].wait()
    pass_c.wait_recv()

    def z_copy(way, hop, w):
        ahead = z_up if way == 0 else z_down
        owner = lax.rem(z + 8 - (hop - 1), 8) if way == 0 else lax.rem(z + hop - 1, 8)
        ref = y_buf.at[w, owner]
        return remote(ref, ref, z_send.at[way, hop - 1, w], z_recv.at[way, hop - 1, w], z=ahead)

    lhs = e_full[quarter[3]].reshape(2 * slots, 512)
    for w in range(2):
        real = acc[2 * w] + dot_t(lhs, w_buf[3, w, 0])
        imag = acc[2 * w + 1] + dot_t(lhs, w_buf[3, w, 1])
        y_buf[w, z, 0] = (real[:slots] - imag[slots:]).astype(BF16)
        y_buf[w, z, 1] = (imag[:slots] + real[slots:]).astype(BF16)
        for way in range(2):
            z_copy(way, 1, w).start()

    def z_pass(hop, w):
        for way in range(2):
            if hop < 4 or way == w:
                z_copy(way, hop, w).wait_recv()
                if hop < 3 or (hop == 3 and way == w):
                    z_copy(way, hop + 1, w).start()

    def x_pass(k):
        for way in range(2):
            x_copy(k, way, 1).wait_recv()
            x_copy(k, way, 2).start()

    x_pass(0)
    remote(other, e_plane.at[:, own_b], a_send, a_recv, yh=1 - yh, yl=1 - yl).wait_recv()
    for way in range(2):
        x_copy(1, way, 1).start()
    z_pass(1, 0)
    x_pass(1)
    z_pass(1, 1)
    for k in range(2):
        for way in range(2):
            x_copy(k, way, 2).wait_recv()

    pair = z // 2
    even = lax.rem(z, 2) == 0

    def products(g):
        def swap(i, carry):
            w, j = i // 2, i % 2
            y_swap[w, j, 0] = y_buf[w, 2 * g + j, 1]
            y_swap[w, j, 1] = -y_buf[w, 2 * g + j, 0]
            return carry

        lax.fori_loop(0, 4, swap, 0)

        def rows(i, carry):
            real = e_plane[0, pl.ds(i * 4, 4)].reshape(4 * slots, 512)
            imag = e_plane[1, pl.ds(i * 4, 4)].reshape(4 * slots, 512)
            total = None
            for w in range(2):
                straight = y_buf[w, pl.ds(2 * g, 2)].reshape(4 * slots, 512)
                swapped = y_swap[w].reshape(4 * slots, 512)
                both = dot_t(real, straight) + dot_t(imag, swapped)
                s = s_col[w, pl.ds(i * 4, 4)].reshape(4 * slots, 128)
                factor = 0.5 * (jnp.concatenate([s, s, s], axis=1) + s_row[w, g][0:1])
                total = both * factor if total is None else total + both * factor
            s_sum[pl.ds(i * 4, 4)] = total.reshape(4, slots, 4 * slots)
            return carry

        lax.fori_loop(0, 2, rows, 0)

    def out_copy(slot, dyh, dx, to_yl):
        to_yh, to_x = lax.rem(yh + dyh, 2), lax.rem(x + dx, 4)
        index = yl * 8 + own_b
        return remote(o_buf.at[slot, to_yh * 4 + to_x], o_recv.at[index], o_send.at[slot, dyh * 4 + dx], o_sem.at[index],
                      yh=to_yh, x=to_x, yl=to_yl)

    places = [lax.rem(pair, 4),
              jnp.where(even, lax.rem(pair + 3, 4), lax.rem(pair + 1, 4)),
              jnp.where(even, lax.rem(pair + 1, 4), lax.rem(pair + 3, 4)),
              lax.rem(pair + 2, 4)]
    slot_of = [0, 0, 1, 1]

    def finish(t):
        g, slot = places[t], slot_of[t]
        products(g)
        mine = lax.rem(g, 2) == c
        across = remote(x_send.at[slot], x_recv.at[slot], d_send.at[slot], d_recv.at[slot], c=1 - c)

        @pl.when(jnp.logical_not(mine))
        def _():
            x_send[slot] = s_sum[...].astype(BF16)
            across.start()

        @pl.when(mine)
        def _():
            across.wait_recv()
            o_buf[slot] = (s_sum[...] + x_recv[slot].astype(F32)).astype(BF16)
            to_yl = g // 2
            for dyh in range(2):
                for dx in range(4):
                    if dyh or dx:
                        out_copy(slot, dyh, dx, to_yl).start()

            @pl.when(to_yl == yl)
            def _():
                o_recv[yl * 8 + own_b] = o_buf[slot, own_b]

            @pl.when(to_yl != yl)
            def _():
                out_copy(slot, 0, 0, to_yl).start()

    finish(0)
    z_pass(2, 0)
    z_pass(2, 1)
    finish(1)
    z_pass(3, 0)
    z_pass(3, 1)
    finish(2)
    z_pass(4, 0)
    z_pass(4, 1)
    finish(3)

    for dyh in range(2):
        for dx in range(4):
            for dyl in range(2):
                if dyh or dx or dyl:
                    index = lax.rem(yl + dyl, 2) * 8 + lax.rem(yh + dyh, 2) * 4 + lax.rem(x + dx, 4)
                    remote(o_buf.at[0, 0], o_recv.at[index], o_send.at[0, 0], o_sem.at[index], c=1 - c).wait_recv()

    for b in range(8):
        block = o_recv[b].astype(F32) + o_recv[8 + b].astype(F32)
        for j in range(2):
            for part in range(2):
                at = (j * 2 + part) * slots
                to = j * 8 * slots + b * slots
                out[part, :, to:to + slots] = block[:, at:at + slots]

    to_y.wait_send()
    to_c.wait_send()
    pass_c.wait_send()
    to_a.wait_send()
    for k in range(2):
        for way in range(2):
            for hop in (1, 2):
                x_copy(k, way, hop).wait_send()
    for way in range(2):
        for hop in range(1, 5):
            for w in range(2):
                if hop < 4 or way == w:
                    z_copy(way, hop, w).wait_send()
    for t in range(4):
        g, slot = places[t], slot_of[t]
        mine = lax.rem(g, 2) == c

        @pl.when(jnp.logical_not(mine))
        def _():
            remote(x_send.at[slot], x_recv.at[slot], d_send.at[slot], d_recv.at[slot], c=1 - c).wait_send()

        @pl.when(mine)
        def _():
            for dyh in range(2):
                for dx in range(4):
                    if dyh or dx:
                        out_copy(slot, dyh, dx, g // 2).wait_send()

            @pl.when(g // 2 != yl)
            def _():
                out_copy(slot, 0, 0, g // 2).wait_send()


def on_device(elements, screened, energies, freq_points, freq_weights, band_of_slot):
    slots = elements.shape[1]
    vmem = pl.BlockSpec(memory_space=pltpu.VMEM)
    smem = pl.BlockSpec(memory_space=pltpu.SMEM)
    anywhere = pl.BlockSpec(memory_space=pl.ANY)
    dma = pltpu.SemaphoreType.DMA
    return pl.pallas_call(
        kernel,
        out_shape=jax.ShapeDtypeStruct((2, slots, 16 * slots), F32),
        in_specs=[anywhere, anywhere, vmem, vmem, smem, smem],
        out_specs=vmem,
        scratch_shapes=[
            pltpu.VMEM((4, 2, slots, 512), BF16),
            pltpu.VMEM((2, 8, slots, 512), BF16),
            pltpu.VMEM((4, 2, 2, 512, 512), BF16),
            pltpu.VMEM((4, 2 * slots, 512), F32),
            pltpu.VMEM((2, 8, 2, slots, 512), BF16),
            pltpu.VMEM((2, 2, 2, slots, 512), BF16),
            pltpu.VMEM((8, slots, 4 * slots), F32),
            pltpu.VMEM((2, 8, slots, 4 * slots), BF16),
            pltpu.VMEM((2, 8, slots, 4 * slots), BF16),
            pltpu.VMEM((2, 8, slots, 4 * slots), BF16),
            pltpu.VMEM((16, slots, 4 * slots), BF16),
            pltpu.VMEM((2, 16, slots, 128), F32),
            pltpu.VMEM((2, 4, 8, 4 * slots), F32),
            dma((6,)), dma((3,)), dma((3,)), dma, dma,
            dma((2, 2, 2)), dma((2, 2, 2)), dma((2, 4, 2)), dma((2, 4, 2)),
            dma((2,)), dma((2,)), dma((2, 8)), dma((16,)),
        ],
        compiler_params=pltpu.CompilerParams(
            collective_id=0, has_side_effects=True, vmem_limit_bytes=60 * 1024 * 1024),
        name="self_energy",
    )(elements, screened, energies.reshape(48, 128), band_of_slot.reshape(64, slots), freq_points, freq_weights)


def solution(mesh):
    torus = Mesh(mesh.devices.reshape(8, 2, 4, 2, 2), ("z", "yh", "x", "yl", "c"))
    return jax.shard_map(
        on_device,
        mesh=torus,
        in_specs=(P(None, BAND, GA), P(None, None, GA, None), P(), P(), P(), P()),
        out_specs=P(None, BAND, GA),
        check_vma=False,
    )
```

time: 344 us -> 74.5 us (0.22)
  the two profiles are of different devices: /device:TPU:1 before, /device:TPU:24 now
where the time goes in v1:
time: 74.5 us; the launch traced here: 74.2 us
  Pallas kernels  70.4 us (94%)
  local copies, waits for them, and re-layouts  3.78 us (5%)
    pallas_call x1, Pallas kernels, on_device(): pl.pallas_call(kernel, out_shape=jax.ShapeDtypeStruct((2, slots, 16 * slo...  70.4 us
    unnamed x1, local copies, waits for them, and re-layouts  2.36 us

profile of v1, /device:TPU:24, one launch (start us, length us, event | category | flops | bytes accessed | tf_op | source)
XLA Modules:
  0.0 74.2 jit_solution(3175216026023389887)
XLA Ops:
  0.0 1.4 %reshape.7.bands = s32[64,96]{1,0:T(8,128)} reshape(s32[6144]{0:T(1024)} %param.11) | data formatting | bytes 49152 | tf_op jit(solution)/shard_map/reshape | solution.py:343
  1.4 70.4 %self_energy.1 = f32[2,96,1536]{2,1,0:T(8,128)} custom-call(bf16[2,96,512]{2,1,0:T(8,128)(2,1)} %elements.1, bf16[2,2,512,2048]{3,2,1,0:T(8,128)(2,1)} %screened.1, f32[48,128]{1,0:T(8,128)} %bitcast.1, s32[64,96]{1,0:T(8,128)} %reshape.7.bands, f32[2]{0:T(128)} %points.1, f32[2]{0:T(128)} %weights.1), custom_call_target="tpu_custom_call" | custom-call | tf_op jit(solution)/shard_map/self_energy/pallas_call | solution.py:317
  71.9 2.4 %copy.8 = f32[2,96,1536]{2,1,0:T(8,128)} copy(f32[2,96,1536]{2,1,0:T(8,128)} %self_energy.1) | data formatting | bytes 2359296

commit v2 on v1

v2 whole, which is shorter than its diff:
```python
import jax
import jax.numpy as jnp
from jax import lax
from jax.experimental import pallas as pl
from jax.experimental.pallas import tpu as pltpu
from jax.sharding import Mesh
from jax.sharding import PartitionSpec as P

BAND = ("z", "yh", "x")
GA = ("yl", "c")
F32 = jnp.float32
BF16 = jnp.bfloat16
scope = jax.named_scope


def dot_t(a, b):
    return lax.dot_general(a, b, (((1,), (1,)), ((), ())), preferred_element_type=F32)


def kernel(
    elements, screened, energies, bands, points, weights, out,
    e_full, e_plane, w_buf, acc, y_buf, y_swap, s_sum, x_send, x_recv, o_buf, o_recv, s_col, s_row,
    energy_buf, band_buf, band_table, point_buf, weight_buf,
    load_sem, p_send, p_recv, a_send, a_recv, xr_send, xr_recv, z_send, z_recv,
    d_send, d_recv, o_send, o_sem,
):
    z, yh, x, yl, c = (lax.axis_index(name) for name in ("z", "yh", "x", "yl", "c"))
    own_q = yl * 2 + c
    own_b = yh * 4 + x
    slots = e_full.shape[2]

    def remote(src, dst, send, recv, **device):
        return pltpu.make_async_remote_copy(
            src_ref=src, dst_ref=dst, send_sem=send, recv_sem=recv,
            device_id=device, device_id_type=pl.DeviceIdType.MESH)

    quarter = [own_q, yl * 2 + (1 - c), (1 - yl) * 2 + c, (1 - yl) * 2 + (1 - c)]
    load_e = pltpu.make_async_copy(elements, e_full.at[own_q], load_sem.at[0])
    load_p = pltpu.make_async_copy(elements, e_plane.at[:, own_b], load_sem.at[1])
    load_e.start()
    load_p.start()
    load_s = [pltpu.make_async_copy(src, dst, load_sem.at[6 + i]) for i, (src, dst) in enumerate(
        ((energies, energy_buf), (bands, band_buf), (points, point_buf), (weights, weight_buf)))]
    load_w = []
    for k in range(4):
        at = pl.multiple_of(quarter[k] * 512, 512)
        load_w.append(pltpu.make_async_copy(screened.at[:, :, :, pl.ds(at, 512)], w_buf.at[k], load_sem.at[2 + k]))
        load_w[k].start()
    for load in load_s:
        load.start()

    barrier = pltpu.get_barrier_semaphore()

    def greet(**device):
        pl.semaphore_signal(barrier, inc=1, device_id=device, device_id_type=pl.DeviceIdType.MESH)

    def plane(dyh, dx, dyl):
        return dict(yh=lax.rem(yh + dyh, 2), x=lax.rem(x + dx, 4), yl=lax.rem(yl + dyl, 2))

    greet(c=1 - c)
    z_up, z_down = lax.rem(z + 1, 8), lax.rem(z + 7, 8)
    greet(z=z_up)
    greet(z=z_down)
    for dyh in range(2):
        for dx in range(4):
            for dyl in range(2):
                if dyh or dx or dyl:
                    greet(**plane(dyh, dx, dyl))
    with scope("enter"):
        pl.semaphore_wait(barrier, 18)
        load_e.wait()

    to_y = remote(e_full.at[own_q], e_full.at[own_q], p_send.at[0], p_recv.at[0], yl=1 - yl)
    to_c = remote(e_full.at[own_q], e_full.at[own_q], p_send.at[1], p_recv.at[1], c=1 - c)
    to_y.start()
    to_c.start()
    load_p.wait()

    x_up, x_down = lax.rem(x + 1, 4), lax.rem(x + 3, 4)

    def block_at(k, at_x):
        return (yh if k == 0 else 1 - yh) * 4 + at_x

    def x_copy(k, way, hop):
        ahead, behind = (x_up, x_down) if way == 0 else (x_down, x_up)
        if hop == 1:
            ref = e_plane.at[:, block_at(k, x)]
        else:
            ref = e_plane.at[way, block_at(k, behind)]
        return remote(ref, ref, xr_send.at[k, way, hop - 1], xr_recv.at[k, way, hop - 1], x=ahead)

    for way in range(2):
        x_copy(0, way, 1).start()

    def accumulate(k, first):
        lhs = e_full[quarter[k]].reshape(2 * slots, 512)

        for i in range(4):
            term = dot_t(lhs, w_buf[k, i // 2, i % 2])
            acc[i] = term if first else acc[i] + term

    with scope("quarter0"):
        load_w[0].wait()
        accumulate(0, True)

    with scope("quarter1"):
        to_c.wait_recv()
        load_w[1].wait()
        accumulate(1, False)

    with scope("wait_y"):
        to_y.wait_recv()
    other = e_full.at[quarter[2]]
    pass_c = remote(other, other, p_send.at[2], p_recv.at[2], c=1 - c)
    pass_c.start()
    to_a = remote(other, e_plane.at[:, own_b], a_send, a_recv, yh=1 - yh, yl=1 - yl)
    to_a.start()
    with scope("quarter2"):
        load_w[2].wait()
        accumulate(2, False)
        load_w[3].wait()
    with scope("wait_c"):
        pass_c.wait_recv()

    def z_copy(way, hop, w):
        ahead = z_up if way == 0 else z_down
        owner = lax.rem(z + 8 - (hop - 1), 8) if way == 0 else lax.rem(z + hop - 1, 8)
        ref = y_buf.at[w, owner]
        return remote(ref, ref, z_send.at[way, hop - 1, w], z_recv.at[way, hop - 1, w], z=ahead)

    with scope("applied"):
        lhs = e_full[quarter[3]].reshape(2 * slots, 512)
        for w in range(2):
            real = acc[2 * w] + dot_t(lhs, w_buf[3, w, 0])
            imag = acc[2 * w + 1] + dot_t(lhs, w_buf[3, w, 1])
            y_buf[w, z, 0] = (real[:slots] - imag[slots:]).astype(BF16)
            y_buf[w, z, 1] = (imag[:slots] + real[slots:]).astype(BF16)
            for way in range(2):
                z_copy(way, 1, w).start()

    def z_pass(hop, w):
        for way in range(2):
            if hop < 4 or way == w:
                z_copy(way, hop, w).wait_recv()
                if hop < 3 or (hop == 3 and way == w):
                    z_copy(way, hop + 1, w).start()

    def x_pass(k):
        for way in range(2):
            x_copy(k, way, 1).wait_recv()
            x_copy(k, way, 2).start()

    def spread_bands():
        rows = [band_buf[pl.ds(k, 16, stride=3), :] for k in range(3)]
        band_table[0] = rows[0]
        band_table[1] = jnp.concatenate([rows[0][:, 96:], rows[1][:, :96]], axis=1)
        band_table[2] = jnp.concatenate([rows[1][:, 64:], rows[2][:, :64]], axis=1)
        band_table[3] = jnp.concatenate([rows[2][:, 32:], rows[2][:, :32]], axis=1)

    def look_up(i, carry):
        at = jnp.where(i < 8, z * 8 + i, (i - 8) * 8 + own_b)
        band = band_table[lax.rem(at, 4), pl.ds(at // 4, 1), :]
        band = jnp.broadcast_to(band, (128, 128)).T[:slots]
        lane = lax.broadcasted_iota(jnp.int32, (slots, 128), 1)

        def part(j, total):
            for u in range(8):
                row = j * 8 + u
                e = jnp.broadcast_to(energy_buf[pl.ds(row, 1), :], (slots, 128))
                total = total + jnp.where(band == lane + row * 128, e, 0.0)
            return total

        total = lax.fori_loop(0, 6, part, jnp.zeros((slots, 128), F32))
        energy = jnp.broadcast_to(jnp.sum(total, axis=1, keepdims=True), (slots, 128))
        for w in range(2):
            offset = energy - point_buf[w]
            s_col[w, i] = weight_buf[w] / (1.0 + 4.0 * offset * offset)
        return carry

    def turn(i, carry):
        w, g = i // 8, lax.rem(i, 8)
        one = s_col[w, 8 + g]
        s_row[w, g] = jnp.concatenate([one, one], axis=0).T[0:8]
        return carry

    with scope("x_pass0"):
        x_pass(0)
    with scope("look_up0"):
        for load in load_s:
            load.wait()
        spread_bands()
        lax.fori_loop(0, 8, look_up, 0)
    with scope("wait_a"):
        remote(other, e_plane.at[:, own_b], a_send, a_recv, yh=1 - yh, yl=1 - yl).wait_recv()
    for way in range(2):
        x_copy(1, way, 1).start()
    with scope("z10"):
        z_pass(1, 0)
    with scope("look_up1"):
        lax.fori_loop(8, 16, look_up, 0)
        lax.fori_loop(0, 16, turn, 0)
    with scope("x_pass1"):
        x_pass(1)
    with scope("z11"):
        z_pass(1, 1)
    with scope("wait_x"):
        for k in range(2):
            for way in range(2):
                x_copy(k, way, 2).wait_recv()

    half = slots // 2
    deltas = (0, 7, 1, 6, 2, 5, 3, 4)

    def block_z(t):
        return lax.rem(z + deltas[t], 8)

    def mine(t):
        return lax.rem(block_z(t) // 2, 2) == c

    def across(t):
        return remote(x_send.at[t], x_recv.at[t], d_send.at[t], d_recv.at[t], c=1 - c)

    @scope("products")
    def products(t):
        zz = block_z(t)
        for w in range(2):
            y_swap[w, 0] = y_buf[w, zz, 1]
            y_swap[w, 1] = -y_buf[w, zz, 0]
        for i in range(2):
            real = e_plane[0, i * 4:i * 4 + 4].reshape(4 * slots, 512)
            imag = e_plane[1, i * 4:i * 4 + 4].reshape(4 * slots, 512)
            total = None
            for w in range(2):
                both = dot_t(real, y_buf[w, zz].reshape(2 * slots, 512)) + dot_t(imag, y_swap[w].reshape(2 * slots, 512))
                s = s_col[w, i * 4:i * 4 + 4].reshape(4 * slots, 128)
                factor = 0.5 * (jnp.concatenate([s, s[:, :2 * slots - 128]], axis=1) + s_row[w, zz][0:1])
                total = both * factor if total is None else total + both * factor
            total = total.reshape(4, slots, 2 * slots)
            s_sum[t % 2, i * 4:i * 4 + 4] = jnp.concatenate([total[:, :half], total[:, half:]], axis=2)

        @pl.when(jnp.logical_not(mine(t)))
        def _():
            x_send[t] = s_sum[t % 2].astype(BF16)
            across(t).start()

    def out_copy(t, dyh, dx):
        zz = block_z(t)
        to_yh, to_x = lax.rem(yh + dyh, 2), lax.rem(x + dx, 4)
        index, column = yl * 8 + own_b, lax.rem(zz, 2)
        return remote(o_buf.at[t, to_yh * 4 + to_x], o_recv.at[column, index], o_send.at[t, dyh * 4 + dx],
                      o_sem.at[column, index], yh=to_yh, x=to_x, yl=zz // 4)

    @scope("complete")
    def complete(t):
        @pl.when(mine(t))
        def _():
            across(t).wait_recv()
            o_buf[t] = (s_sum[t % 2] + x_recv[t].astype(F32)).astype(BF16)
            for dx in (2, 1, 3, 0):
                for dyh in (1, 0):
                    if dyh or dx:
                        out_copy(t, dyh, dx).start()

            @pl.when(block_z(t) // 4 == yl)
            def _():
                o_recv[lax.rem(block_z(t), 2), yl * 8 + own_b] = o_buf[t, own_b]

            @pl.when(block_z(t) // 4 != yl)
            def _():
                out_copy(t, 0, 0).start()

    products(0)
    z_pass(2, 0)
    products(1)
    complete(0)
    with scope("z21"):
        z_pass(2, 1)
    products(2)
    complete(1)
    products(3)
    complete(2)
    with scope("z30"):
        z_pass(3, 0)
    products(4)
    complete(3)
    with scope("z31"):
        z_pass(3, 1)
    products(5)
    complete(4)
    products(6)
    complete(5)
    with scope("z40"):
        z_pass(4, 0)
    complete(6)
    with scope("z41"):
        z_pass(4, 1)
    products(7)
    complete(7)

    with scope("wait_out"):
        for column in range(2):
            for dyh in range(2):
                for dx in range(4):
                    for dyl in range(2):
                        if dyh or dx or dyl:
                            index = lax.rem(yl + dyl, 2) * 8 + lax.rem(yh + dyh, 2) * 4 + lax.rem(x + dx, 4)
                            remote(o_buf.at[0, 0], o_recv.at[column, index], o_send.at[0, 0],
                                   o_sem.at[column, index], c=1 - c).wait_recv()

    with scope("lay_out"):
        for column in range(2):
            for b in range(8):
                block = o_recv[column, b].astype(F32) + o_recv[column, 8 + b].astype(F32)
                to = (column * 8 + b) * slots
                for part in range(2):
                    for low in range(2):
                        at = (low * 2 + part) * slots
                        out[part, low * half:low * half + half, to:to + slots] = block[:, at:at + slots]

    to_y.wait_send()
    to_c.wait_send()
    pass_c.wait_send()
    to_a.wait_send()
    for k in range(2):
        for way in range(2):
            for hop in (1, 2):
                x_copy(k, way, hop).wait_send()
    for way in range(2):
        for hop in range(1, 5):
            for w in range(2):
                if hop < 4 or way == w:
                    z_copy(way, hop, w).wait_send()
    for t in range(8):
        @pl.when(jnp.logical_not(mine(t)))
        def _():
            across(t).wait_send()

        @pl.when(mine(t))
        def _():
            for dyh in range(2):
                for dx in range(4):
                    if dyh or dx:
                        out_copy(t, dyh, dx).wait_send()

            @pl.when(block_z(t) // 4 != yl)
            def _():
                out_copy(t, 0, 0).wait_send()


def on_device(elements, screened, energies, freq_points, freq_weights, band_of_slot):
    slots = elements.shape[1]
    half = slots // 2
    vmem = pl.BlockSpec(memory_space=pltpu.VMEM)
    anywhere = pl.BlockSpec(memory_space=pl.ANY)
    dma = pltpu.SemaphoreType.DMA
    return pl.pallas_call(
        kernel,
        out_shape=jax.ShapeDtypeStruct((2, slots, 16 * slots), F32),
        in_specs=[anywhere] * 6,
        out_specs=vmem,
        scratch_shapes=[
            pltpu.VMEM((4, 2, slots, 512), BF16),
            pltpu.VMEM((2, 8, slots, 512), BF16),
            pltpu.VMEM((4, 2, 2, 512, 512), BF16),
            pltpu.VMEM((4, 2 * slots, 512), F32),
            pltpu.VMEM((2, 8, 2, slots, 512), BF16),
            pltpu.VMEM((2, 2, slots, 512), BF16),
            pltpu.VMEM((2, 8, half, 4 * slots), F32),
            pltpu.VMEM((8, 8, half, 4 * slots), BF16),
            pltpu.VMEM((8, 8, half, 4 * slots), BF16),
            pltpu.VMEM((8, 8, half, 4 * slots), BF16),
            pltpu.VMEM((2, 16, half, 4 * slots), BF16),
            pltpu.VMEM((2, 16, slots, 128), F32),
            pltpu.VMEM((2, 8, 8, 2 * slots), F32),
            pltpu.VMEM((48, 128), F32),
            pltpu.VMEM((48, 128), jnp.int32),
            pltpu.VMEM((4, 16, 128), jnp.int32),
            pltpu.SMEM((2,), F32), pltpu.SMEM((2,), F32),
            dma((10,)), dma((3,)), dma((3,)), dma, dma,
            dma((2, 2, 2)), dma((2, 2, 2)), dma((2, 4, 2)), dma((2, 4, 2)),
            dma((8,)), dma((8,)), dma((8, 8)), dma((2, 16)),
        ],
        compiler_params=pltpu.CompilerParams(
            collective_id=0, has_side_effects=True, vmem_limit_bytes=60 * 1024 * 1024),
        name="self_energy",
    )(elements, screened, energies.reshape(48, 128), band_of_slot.reshape(48, 128), freq_points, freq_weights)


def solution(mesh):
    torus = Mesh(mesh.devices.reshape(8, 2, 4, 2, 2), ("z", "yh", "x", "yl", "c"))
    return jax.shard_map(
        on_device,
        mesh=torus,
        in_specs=(P(None, BAND, GA), P(None, None, GA, None), P(), P(), P(), P()),
        out_specs=P(None, BAND, GA),
        check_vma=False,
    )
```

time: 74.5 us -> 63.9 us (0.86)
  the two profiles are of different devices: /device:TPU:24 before, /device:TPU:89 now
where the time goes in v2:
time: 63.9 us; the launch traced here: 63.8 us
  Pallas kernels  61.4 us (96%)
  local copies, waits for them, and re-layouts  2.36 us (4%)
    pallas_call x1, Pallas kernels, on_device(): pl.pallas_call(kernel, out_shape=jax.ShapeDtypeStruct((2, slots, 16 * slo...  61.4 us
    unnamed x1, local copies, waits for them, and re-layouts  2.36 us

profile of v2, /device:TPU:89, one launch (start us, length us, event | category | flops | bytes accessed | tf_op | source)
XLA Modules:
  0.0 63.8 jit_solution(14263139917017310016)
XLA Ops:
  0.0 61.4 %self_energy.1 = f32[2,96,1536]{2,1,0:T(8,128)} custom-call(bf16[2,96,512]{2,1,0:T(8,128)(2,1)} %elements.1, bf16[2,2,512,2048]{3,2,1,0:T(8,128)(2,1)} %screened.1, f32[48,128]{1,0:T(8,128)} %bitcast.2, s32[48,128]{1,0:T(8,128)} %bitcast.3, f32[2]{0:T(128)} %points.1, f32[2]{0:T(128)} %weights.1), custom_call_target="tpu_custom_call" | custom-call | tf_op jit(solution)/shard_map/self_energy/pallas_call | solution.py:356
  61.4 2.4 %copy.8 = f32[2,96,1536]{2,1,0:T(8,128)} copy(f32[2,96,1536]{2,1,0:T(8,128)} %self_energy.1) | data formatting | bytes 2359296

commit v3 on v2

--- a/solution.py
+++ b/solution.py
@@ -18,10 +18,10 @@
 
 
 def kernel(
-    elements, screened, energies, bands, points, weights, out,
-    e_full, e_plane, w_buf, acc, y_buf, y_swap, s_sum, x_send, x_recv, o_buf, o_recv, s_col, s_row,
+    elements, screened, energies, bands, points, weights, o_recv,
+    e_full, e_plane, w_buf, acc, y_buf, y_swap, s_sum, x_send, x_recv, o_buf, s_col, s_row,
     energy_buf, band_buf, band_table, point_buf, weight_buf,
-    load_sem, p_send, p_recv, a_send, a_recv, xr_send, xr_recv, z_send, z_recv,
+    load_sem, keep_sem, p_send, p_recv, a_send, a_recv, xr_send, xr_recv, z_send, z_recv,
     d_send, d_recv, o_send, o_sem,
 ):
     z, yh, x, yl, c = (lax.axis_index(name) for name in ("z", "yh", "x", "yl", "c"))
@@ -61,18 +61,21 @@
     z_up, z_down = lax.rem(z + 1, 8), lax.rem(z + 7, 8)
     greet(z=z_up)
     greet(z=z_down)
-    for dyh in range(2):
-        for dx in range(4):
-            for dyl in range(2):
-                if dyh or dx or dyl:
-                    greet(**plane(dyh, dx, dyl))
+    greet(yl=1 - yl)
+    greet(yh=1 - yh, yl=1 - yl)
+    greet(x=lax.rem(x + 1, 4))
+    greet(x=lax.rem(x + 3, 4))
     with scope("enter"):
-        pl.semaphore_wait(barrier, 18)
+        pl.semaphore_wait(barrier, 7)
         load_e.wait()
 
-    to_y = remote(e_full.at[own_q], e_full.at[own_q], p_send.at[0], p_recv.at[0], yl=1 - yl)
-    to_c = remote(e_full.at[own_q], e_full.at[own_q], p_send.at[1], p_recv.at[1], c=1 - c)
-    to_y.start()
+    def to_y(h):
+        ref = e_full.at[own_q, :, :, pl.ds(h * 256, 256)]
+        return remote(ref, ref, p_send.at[2 * h], p_recv.at[2 * h], yl=1 - yl)
+
+    to_c = remote(e_full.at[own_q], e_full.at[own_q], p_send.at[4], p_recv.at[4], c=1 - c)
+    to_y(0).start()
+    to_y(1).start()
     to_c.start()
     load_p.wait()
 
@@ -92,35 +95,47 @@
     for way in range(2):
         x_copy(0, way, 1).start()
 
-    def accumulate(k, first):
-        lhs = e_full[quarter[k]].reshape(2 * slots, 512)
-
+    def terms(k, w, part, low, size):
+        lhs = e_full[quarter[k], :, :, low:low + size].reshape(2 * slots, size)
+        return dot_t(lhs, w_buf[k, w, part, :, low:low + size])
+
+    def accumulate(k, low=0, size=512):
         for i in range(4):
-            term = dot_t(lhs, w_buf[k, i // 2, i % 2])
-            acc[i] = term if first else acc[i] + term
+            term = terms(k, i // 2, i % 2, low, size)
+            acc[i] = term if k == 0 else acc[i] + term
 
     with scope("quarter0"):
         load_w[0].wait()
-        accumulate(0, True)
+        accumulate(0)
 
     with scope("quarter1"):
         to_c.wait_recv()
         load_w[1].wait()
-        accumulate(1, False)
-
-    with scope("wait_y"):
-        to_y.wait_recv()
+        accumulate(1)
+
+    def pass_c(h):
+        ref = e_full.at[quarter[2], :, :, pl.ds(h * 256, 256)]
+        return remote(ref, ref, p_send.at[2 * h + 1], p_recv.at[2 * h + 1], c=1 - c)
+
     other = e_full.at[quarter[2]]
-    pass_c = remote(other, other, p_send.at[2], p_recv.at[2], c=1 - c)
-    pass_c.start()
     to_a = remote(other, e_plane.at[:, own_b], a_send, a_recv, yh=1 - yh, yl=1 - yl)
+    load_w[2].wait()
+    load_w[3].wait()
+    with scope("wait_y0"):
+        to_y(0).wait_recv()
+    pass_c(0).start()
+    with scope("quarter2"):
+        accumulate(2, 0, 256)
+    with scope("wait_y1"):
+        to_y(1).wait_recv()
+    pass_c(1).start()
     to_a.start()
-    with scope("quarter2"):
-        load_w[2].wait()
-        accumulate(2, False)
-        load_w[3].wait()
+    with scope("quarter3"):
+        accumulate(2, 256, 256)
+        pass_c(0).wait_recv()
+        accumulate(3, 0, 256)
     with scope("wait_c"):
-        pass_c.wait_recv()
+        pass_c(1).wait_recv()
 
     def z_copy(way, hop, w):
         ahead = z_up if way == 0 else z_down
@@ -129,21 +144,23 @@
         return remote(ref, ref, z_send.at[way, hop - 1, w], z_recv.at[way, hop - 1, w], z=ahead)
 
     with scope("applied"):
-        lhs = e_full[quarter[3]].reshape(2 * slots, 512)
         for w in range(2):
-            real = acc[2 * w] + dot_t(lhs, w_buf[3, w, 0])
-            imag = acc[2 * w + 1] + dot_t(lhs, w_buf[3, w, 1])
+            real = acc[2 * w] + terms(3, w, 0, 256, 256)
+            imag = acc[2 * w + 1] + terms(3, w, 1, 256, 256)
             y_buf[w, z, 0] = (real[:slots] - imag[slots:]).astype(BF16)
             y_buf[w, z, 1] = (imag[:slots] + real[slots:]).astype(BF16)
-            for way in range(2):
-                z_copy(way, 1, w).start()
-
-    def z_pass(hop, w):
+            if w == 0:
+                z_copy(0, 1, 0).start()
+        z_copy(1, 1, 1).start()
+        z_copy(0, 1, 1).start()
+        z_copy(1, 1, 0).start()
+
+    def z_pass(hop, turn):
         for way in range(2):
-            if hop < 4 or way == w:
-                z_copy(way, hop, w).wait_recv()
-                if hop < 3 or (hop == 3 and way == w):
-                    z_copy(way, hop + 1, w).start()
+            w = turn if way == 0 else 1 - turn
+            z_copy(way, hop, w).wait_recv()
+            if hop < 3 or (hop == 3 and turn == 0):
+                z_copy(way, hop + 1, w).start()
 
     def x_pass(k):
         for way in range(2):
@@ -198,11 +215,14 @@
         z_pass(1, 0)
     with scope("look_up1"):
         lax.fori_loop(8, 16, look_up, 0)
-        lax.fori_loop(0, 16, turn, 0)
     with scope("x_pass1"):
         x_pass(1)
     with scope("z11"):
         z_pass(1, 1)
+    with scope("turn"):
+        lax.fori_loop(0, 16, turn, 0)
+    with scope("z20"):
+        z_pass(2, 0)
     with scope("wait_x"):
         for k in range(2):
             for way in range(2):
@@ -250,6 +270,9 @@
         return remote(o_buf.at[t, to_yh * 4 + to_x], o_recv.at[column, index], o_send.at[t, dyh * 4 + dx],
                       o_sem.at[column, index], yh=to_yh, x=to_x, yl=zz // 4)
 
+    def keep(t):
+        return pltpu.make_async_copy(o_buf.at[t, own_b], o_recv.at[lax.rem(block_z(t), 2), yl * 8 + own_b], keep_sem.at[t])
+
     @scope("complete")
     def complete(t):
         @pl.when(mine(t))
@@ -263,24 +286,23 @@
 
             @pl.when(block_z(t) // 4 == yl)
             def _():
-                o_recv[lax.rem(block_z(t), 2), yl * 8 + own_b] = o_buf[t, own_b]
+                keep(t).start()
 
             @pl.when(block_z(t) // 4 != yl)
             def _():
                 out_copy(t, 0, 0).start()
 
     products(0)
-    z_pass(2, 0)
     products(1)
     complete(0)
     with scope("z21"):
         z_pass(2, 1)
     products(2)
     complete(1)
+    with scope("z30"):
+        z_pass(3, 0)
     products(3)
     complete(2)
-    with scope("z30"):
-        z_pass(3, 0)
     products(4)
     complete(3)
     with scope("z31"):
@@ -289,11 +311,9 @@
     complete(4)
     products(6)
     complete(5)
+    complete(6)
     with scope("z40"):
         z_pass(4, 0)
-    complete(6)
-    with scope("z41"):
-        z_pass(4, 1)
     products(7)
     complete(7)
 
@@ -307,57 +327,80 @@
                             remote(o_buf.at[0, 0], o_recv.at[column, index], o_send.at[0, 0],
                                    o_sem.at[column, index], c=1 - c).wait_recv()
 
-    with scope("lay_out"):
-        for column in range(2):
-            for b in range(8):
-                block = o_recv[column, b].astype(F32) + o_recv[column, 8 + b].astype(F32)
-                to = (column * 8 + b) * slots
-                for part in range(2):
-                    for low in range(2):
-                        at = (low * 2 + part) * slots
-                        out[part, low * half:low * half + half, to:to + slots] = block[:, at:at + slots]
-
-    to_y.wait_send()
-    to_c.wait_send()
-    pass_c.wait_send()
-    to_a.wait_send()
-    for k in range(2):
+    with scope("drain"):
+        to_c.wait_send()
+        for h in range(2):
+            to_y(h).wait_send()
+            pass_c(h).wait_send()
+        to_a.wait_send()
+        for k in range(2):
+            for way in range(2):
+                for hop in (1, 2):
+                    x_copy(k, way, hop).wait_send()
         for way in range(2):
-            for hop in (1, 2):
-                x_copy(k, way, hop).wait_send()
-    for way in range(2):
-        for hop in range(1, 5):
-            for w in range(2):
-                if hop < 4 or way == w:
-                    z_copy(way, hop, w).wait_send()
-    for t in range(8):
-        @pl.when(jnp.logical_not(mine(t)))
-        def _():
-            across(t).wait_send()
-
-        @pl.when(mine(t))
-        def _():
-            for dyh in range(2):
-                for dx in range(4):
-                    if dyh or dx:
-                        out_copy(t, dyh, dx).wait_send()
-
-            @pl.when(block_z(t) // 4 != yl)
+            for hop in range(1, 5):
+                for w in range(2):
+                    if hop < 4 or way == w:
+                        z_copy(way, hop, w).wait_send()
+        for t in range(8):
+            @pl.when(jnp.logical_not(mine(t)))
             def _():
-                out_copy(t, 0, 0).wait_send()
+                across(t).wait_send()
+
+            @pl.when(mine(t))
+            def _():
+                for dyh in range(2):
+                    for dx in range(4):
+                        if dyh or dx:
+                            out_copy(t, dyh, dx).wait_send()
+
+                @pl.when(block_z(t) // 4 == yl)
+                def _():
+                    keep(t).wait()
+
+                @pl.when(block_z(t) // 4 != yl)
+                def _():
+                    out_copy(t, 0, 0).wait_send()
+
+
+def lay_out(parts, out, held, laid, in_sem, out_sem):
+    rows = laid.shape[2]
+    half = rows // 2
+    loads, stores = [], []
+    for i in range(4):
+        column, low = i // 2, i % 2 * 4
+        for side in range(2):
+            loads.append(pltpu.make_async_copy(
+                parts.at[column, pl.ds(side * 8 + low, 4)], held.at[i, side], in_sem.at[i, side]))
+            loads[-1].start()
+        stores.append(pltpu.make_async_copy(
+            laid.at[i], out.at[:, :, pl.ds(i * 4 * rows, 4 * rows)], out_sem.at[i]))
+    for i in range(4):
+        with scope("held"):
+            loads[2 * i].wait()
+            loads[2 * i + 1].wait()
+        for b in range(4):
+            block = held[i, 0, b].astype(F32) + held[i, 1, b].astype(F32)
+            for part in range(2):
+                for side in range(2):
+                    at = (side * 2 + part) * rows
+                    laid[i, part, side * half:side * half + half, b * rows:b * rows + rows] = block[:, at:at + rows]
+        stores[i].start()
+    with scope("stored"):
+        for store in stores:
+            store.wait()
 
 
 def on_device(elements, screened, energies, freq_points, freq_weights, band_of_slot):
     slots = elements.shape[1]
     half = slots // 2
-    vmem = pl.BlockSpec(memory_space=pltpu.VMEM)
     anywhere = pl.BlockSpec(memory_space=pl.ANY)
     dma = pltpu.SemaphoreType.DMA
-    return pl.pallas_call(
+    parts = pl.pallas_call(
         kernel,
-        out_shape=jax.ShapeDtypeStruct((2, slots, 16 * slots), F32),
+        out_shape=jax.ShapeDtypeStruct((2, 16, half, 4 * slots), BF16),
         in_specs=[anywhere] * 6,
-        out_specs=vmem,
+        out_specs=anywhere,
         scratch_shapes=[
             pltpu.VMEM((4, 2, slots, 512), BF16),
             pltpu.VMEM((2, 8, slots, 512), BF16),
@@ -369,14 +412,13 @@
             pltpu.VMEM((8, 8, half, 4 * slots), BF16),
             pltpu.VMEM((8, 8, half, 4 * slots), BF16),
             pltpu.VMEM((8, 8, half, 4 * slots), BF16),
-            pltpu.VMEM((2, 16, half, 4 * slots), BF16),
             pltpu.VMEM((2, 16, slots, 128), F32),
             pltpu.VMEM((2, 8, 8, 2 * slots), F32),
             pltpu.VMEM((48, 128), F32),
             pltpu.VMEM((48, 128), jnp.int32),
             pltpu.VMEM((4, 16, 128), jnp.int32),
             pltpu.SMEM((2,), F32), pltpu.SMEM((2,), F32),
-            dma((10,)), dma((3,)), dma((3,)), dma, dma,
+            dma((10,)), dma((8,)), dma((5,)), dma((5,)), dma, dma,
             dma((2, 2, 2)), dma((2, 2, 2)), dma((2, 4, 2)), dma((2, 4, 2)),
             dma((8,)), dma((8,)), dma((8, 8)), dma((2, 16)),
         ],
@@ -384,6 +426,19 @@
             collective_id=0, has_side_effects=True, vmem_limit_bytes=60 * 1024 * 1024),
         name="self_energy",
     )(elements, screened, energies.reshape(48, 128), band_of_slot.reshape(48, 128), freq_points, freq_weights)
+    return pl.pallas_call(
+        lay_out,
+        out_shape=jax.ShapeDtypeStruct((2, slots, 16 * slots), F32),
+        in_specs=[anywhere],
+        out_specs=anywhere,
+        scratch_shapes=[
+            pltpu.VMEM((4, 2, 4, half, 4 * slots), BF16),
+            pltpu.VMEM((4, 2, slots, 4 * slots), F32),
+            dma((4, 2)), dma((4,)),
+        ],
+        compiler_params=pltpu.CompilerParams(vmem_limit_bytes=60 * 1024 * 1024),
+        name="lay_out",
+    )(parts)
 
 
 def solution(mesh):

time: 63.9 us -> 61.3 us (0.959)
  the two profiles are of different devices: /device:TPU:89 before, /device:TPU:73 now
where the time goes in v3:
time: 61.3 us; the launch traced here: 61.2 us
  Pallas kernels  61.1 us (100%)
    pallas_call x1, Pallas kernels, on_device(): pl.pallas_call(kernel, out_shape=jax.ShapeDtypeStruct((2, 16, half, 4 * s...  58.6 us
    pallas_call x1, Pallas kernels, on_device(): pl.pallas_call(lay_out, out_shape=jax.ShapeDtypeStruct((2, slots, 16 * sl...  2.54 us

profile of v3, /device:TPU:73, one launch (start us, length us, event | category | flops | bytes accessed | tf_op | source)
XLA Modules:
  0.0 61.2 jit_solution(11684595294251716147)
XLA Ops:
  0.0 58.6 %self_energy.1.parts = bf16[2,16,48,384]{3,2,1,0:T(8,128)(2,1)} custom-call(bf16[2,96,512]{2,1,0:T(8,128)(2,1)} %elements.1, bf16[2,2,512,2048]{3,2,1,0:T(8,128)(2,1)} %screened.1, f32[48,128]{1,0:T(8,128)} %bitcast.2, s32[48,128]{1,0:T(8,128)} %bitcast.3, f32[2]{0:T(128)} %points.1, f32[2]{0:T(128)} %weights.1), custom_call_target="tpu_custom_call" | custom-call | tf_op jit(solution)/shard_map/self_energy/pallas_call | solution.py:399
  58.6 2.5 %lay_out.1 = f32[2,96,1536]{2,1,0:T(8,128)} custom-call(bf16[2,16,48,384]{3,2,1,0:T(8,128)(2,1)} %self_energy.1.parts), custom_call_target="tpu_custom_call" | custom-call | tf_op jit(solution)/shard_map/lay_out/pallas_call | solution.py:429

commit v4 on v3

--- a/solution.py
+++ b/solution.py
@@ -19,10 +19,10 @@
 
 def kernel(
     elements, screened, energies, bands, points, weights, o_recv,
-    e_full, e_plane, w_buf, acc, y_buf, y_swap, s_sum, x_send, x_recv, o_buf, s_col, s_row,
+    e_full, e_plane, w_buf, acc, y_buf, y_swap, s_sum, x_send, x_recv, h_send, h_recv, h_keep, o_buf, last_buf, s_col, s_row,
     energy_buf, band_buf, band_table, point_buf, weight_buf,
-    load_sem, keep_sem, p_send, p_recv, a_send, a_recv, xr_send, xr_recv, z_send, z_recv,
-    d_send, d_recv, o_send, o_sem,
+    load_sem, p_send, p_recv, a_recv, xr_send, xr_recv, z_send, z_recv,
+    d_send, d_recv, hs_send, hs_recv, keep_sem, o_send, o_sem, last_send, last_sem,
 ):
     z, yh, x, yl, c = (lax.axis_index(name) for name in ("z", "yh", "x", "yl", "c"))
     own_q = yl * 2 + c
@@ -71,9 +71,9 @@
 
     def to_y(h):
         ref = e_full.at[own_q, :, :, pl.ds(h * 256, 256)]
-        return remote(ref, ref, p_send.at[2 * h], p_recv.at[2 * h], yl=1 - yl)
-
-    to_c = remote(e_full.at[own_q], e_full.at[own_q], p_send.at[4], p_recv.at[4], c=1 - c)
+        return remote(ref, ref, p_send, p_recv.at[2 * h], yl=1 - yl)
+
+    to_c = remote(e_full.at[own_q], e_full.at[own_q], p_send, p_recv.at[4], c=1 - c)
     to_y(0).start()
     to_y(1).start()
     to_c.start()
@@ -90,7 +90,7 @@
             ref = e_plane.at[:, block_at(k, x)]
         else:
             ref = e_plane.at[way, block_at(k, behind)]
-        return remote(ref, ref, xr_send.at[k, way, hop - 1], xr_recv.at[k, way, hop - 1], x=ahead)
+        return remote(ref, ref, xr_send, xr_recv.at[k, way, hop - 1], x=ahead)
 
     for way in range(2):
         x_copy(0, way, 1).start()
@@ -115,10 +115,10 @@
 
     def pass_c(h):
         ref = e_full.at[quarter[2], :, :, pl.ds(h * 256, 256)]
-        return remote(ref, ref, p_send.at[2 * h + 1], p_recv.at[2 * h + 1], c=1 - c)
+        return remote(ref, ref, p_send, p_recv.at[2 * h + 1], c=1 - c)
 
     other = e_full.at[quarter[2]]
-    to_a = remote(other, e_plane.at[:, own_b], a_send, a_recv, yh=1 - yh, yl=1 - yl)
+    to_a = remote(other, e_plane.at[:, own_b], p_send, a_recv, yh=1 - yh, yl=1 - yl)
     load_w[2].wait()
     load_w[3].wait()
     with scope("wait_y0"):
@@ -141,7 +141,7 @@
         ahead = z_up if way == 0 else z_down
         owner = lax.rem(z + 8 - (hop - 1), 8) if way == 0 else lax.rem(z + hop - 1, 8)
         ref = y_buf.at[w, owner]
-        return remote(ref, ref, z_send.at[way, hop - 1, w], z_recv.at[way, hop - 1, w], z=ahead)
+        return remote(ref, ref, z_send, z_recv.at[way, hop - 1, w], z=ahead)
 
     with scope("applied"):
         for w in range(2):
@@ -208,7 +208,7 @@
         spread_bands()
         lax.fori_loop(0, 8, look_up, 0)
     with scope("wait_a"):
-        remote(other, e_plane.at[:, own_b], a_send, a_recv, yh=1 - yh, yl=1 - yl).wait_recv()
+        remote(other, e_plane.at[:, own_b], p_send, a_recv, yh=1 - yh, yl=1 - yl).wait_recv()
     for way in range(2):
         x_copy(1, way, 1).start()
     with scope("z10"):
@@ -238,7 +238,7 @@
         return lax.rem(block_z(t) // 2, 2) == c
 
     def across(t):
-        return remote(x_send.at[t], x_recv.at[t], d_send.at[t], d_recv.at[t], c=1 - c)
+        return remote(x_send.at[t], x_recv.at[t], d_send, d_recv.at[t], c=1 - c)
 
     @scope("products")
     def products(t):
@@ -263,131 +263,191 @@
             x_send[t] = s_sum[t % 2].astype(BF16)
             across(t).start()
 
-    def out_copy(t, dyh, dx):
-        zz = block_z(t)
-        to_yh, to_x = lax.rem(yh + dyh, 2), lax.rem(x + dx, 4)
-        index, column = yl * 8 + own_b, lax.rem(zz, 2)
-        return remote(o_buf.at[t, to_yh * 4 + to_x], o_recv.at[column, index], o_send.at[t, dyh * 4 + dx],
-                      o_sem.at[column, index], yh=to_yh, x=to_x, yl=zz // 4)
-
-    def keep(t):
-        return pltpu.make_async_copy(o_buf.at[t, own_b], o_recv.at[lax.rem(block_z(t), 2), yl * 8 + own_b], keep_sem.at[t])
+    def same_yl(t):
+        return block_z(t) // 4 == yl
+
+    def rows_of(t):
+        return jnp.where(same_yl(t), yh, 1 - yh)
+
+    def partner(t):
+        return remote(h_send.at[t], h_recv.at[t], hs_send, hs_recv.at[t], yl=1 - yl)
+
+    @scope("reduce")
+    def reduce(t):
+        @pl.when(mine(t))
+        def _():
+            across(t).wait_recv()
+            here = rows_of(t) * 4
+            there = 4 - here
+            h_send[t] = (s_sum[t % 2, pl.ds(there, 4)] + x_recv[t, pl.ds(there, 4)].astype(F32)).astype(BF16)
+            partner(t).start()
+            h_keep[t % 2] = s_sum[t % 2, pl.ds(here, 4)] + x_recv[t, pl.ds(here, 4)].astype(F32)
+
+    def out_copy(t, dx):
+        to_x = lax.rem(x + dx, 4)
+        return remote(o_buf.at[t * 4 + to_x], o_recv.at[lax.rem(block_z(t), 2) * 16 + own_b], o_send, o_sem,
+                      x=to_x, yh=rows_of(t), yl=jnp.where(same_yl(t), yl, 1 - yl))
+
+    def keep(src, t):
+        return pltpu.make_async_copy(src, o_recv.at[lax.rem(block_z(t), 2) * 16 + own_b], keep_sem)
 
     @scope("complete")
     def complete(t):
         @pl.when(mine(t))
         def _():
-            across(t).wait_recv()
-            o_buf[t] = (s_sum[t % 2] + x_recv[t].astype(F32)).astype(BF16)
-            for dx in (2, 1, 3, 0):
-                for dyh in (1, 0):
-                    if dyh or dx:
-                        out_copy(t, dyh, dx).start()
-
-            @pl.when(block_z(t) // 4 == yl)
+            partner(t).wait_recv()
+            o_buf[t * 4:t * 4 + 4] = (h_keep[t % 2] + h_recv[t].astype(F32)).astype(BF16)
+            for dx in (2, 1, 3):
+                out_copy(t, dx).start()
+
+            @pl.when(same_yl(t))
             def _():
-                keep(t).start()
-
-            @pl.when(block_z(t) // 4 != yl)
+                keep(o_buf.at[t * 4 + x], t).start()
+
+            @pl.when(jnp.logical_not(same_yl(t)))
             def _():
-                out_copy(t, 0, 0).start()
+                out_copy(t, 0).start()
+
+    last = len(deltas) - 1
+
+    def last_copy(dyh, dx, same):
+        to_yh, to_x = lax.rem(yh + dyh, 2), lax.rem(x + dx, 4)
+        index = lax.rem(block_z(last), 2) * 16 + own_b + (0 if same else 8)
+        return remote(last_buf.at[to_yh * 4 + to_x], o_recv.at[index], last_send, last_sem.at[0 if same else 1],
+                      yh=to_yh, x=to_x, yl=yl if same else 1 - yl)
+
+    @scope("finish")
+    def finish():
+        @pl.when(mine(last))
+        def _():
+            across(last).wait_recv()
+            last_buf[...] = (s_sum[last % 2] + x_recv[last].astype(F32)).astype(BF16)
+            for same in (True, False):
+                @pl.when(same_yl(last) == same)
+                def _():
+                    for dx in (2, 1, 3, 0):
+                        for dyh in (1, 0):
+                            if dx or dyh or not same:
+                                last_copy(dyh, dx, same).start()
+                    if same:
+                        keep(last_buf.at[own_b], last).start()
 
     products(0)
     products(1)
-    complete(0)
+    reduce(0)
+    reduce(1)
     with scope("z21"):
         z_pass(2, 1)
     products(2)
+    complete(0)
     complete(1)
+    reduce(2)
     with scope("z30"):
         z_pass(3, 0)
     products(3)
+    products(4)
     complete(2)
-    products(4)
-    complete(3)
+    reduce(3)
+    reduce(4)
     with scope("z31"):
         z_pass(3, 1)
     products(5)
+    products(6)
+    complete(3)
     complete(4)
-    products(6)
-    complete(5)
-    complete(6)
+    reduce(5)
+    reduce(6)
     with scope("z40"):
         z_pass(4, 0)
     products(7)
-    complete(7)
+    finish()
+    complete(5)
+    complete(6)
+
+    def drain(ref, sem):
+        remote(ref, ref, sem, sem, c=1 - c).wait_send()
 
     with scope("wait_out"):
-        for column in range(2):
-            for dyh in range(2):
-                for dx in range(4):
-                    for dyl in range(2):
-                        if dyh or dx or dyl:
-                            index = lax.rem(yl + dyl, 2) * 8 + lax.rem(yh + dyh, 2) * 4 + lax.rem(x + dx, 4)
-                            remote(o_buf.at[0, 0], o_recv.at[column, index], o_send.at[0, 0],
-                                   o_sem.at[column, index], c=1 - c).wait_recv()
-
-    with scope("drain"):
-        to_c.wait_send()
-        for h in range(2):
-            to_y(h).wait_send()
-            pass_c(h).wait_send()
-        to_a.wait_send()
-        for k in range(2):
-            for way in range(2):
-                for hop in (1, 2):
-                    x_copy(k, way, hop).wait_send()
-        for way in range(2):
-            for hop in range(1, 5):
-                for w in range(2):
-                    if hop < 4 or way == w:
-                        z_copy(way, hop, w).wait_send()
-        for t in range(8):
-            @pl.when(jnp.logical_not(mine(t)))
-            def _():
-                across(t).wait_send()
-
-            @pl.when(mine(t))
-            def _():
-                for dyh in range(2):
-                    for dx in range(4):
-                        if dyh or dx:
-                            out_copy(t, dyh, dx).wait_send()
-
-                @pl.when(block_z(t) // 4 == yl)
+        drain(e_full, p_send)
+        drain(e_plane.at[:, 0:6], xr_send)
+        drain(y_buf.at[:, 0:7], z_send)
+        drain(x_send.at[0:4], d_send)
+        keep(o_buf.at[0], 0).wait()
+        keep(o_buf.at[0], 0).wait()
+
+        @pl.when(jnp.logical_not(mine(last)))
+        def _():
+            drain(h_send.at[0:4], hs_send)
+            drain(o_buf.at[0:14], o_send)
+
+        @pl.when(mine(last))
+        def _():
+            drain(h_send.at[0:3], hs_send)
+            for same in (True, False):
+                @pl.when(same_yl(last) == same)
                 def _():
-                    keep(t).wait()
-
-                @pl.when(block_z(t) // 4 != yl)
-                def _():
-                    out_copy(t, 0, 0).wait_send()
+                    drain(o_buf.at[0:11 if same else 10], o_send)
+                    drain(last_buf.at[0:7 if same else 8], last_send)
+
+        drain_in = lambda n, sem: remote(o_recv.at[0:n], o_recv.at[0:n], o_send, sem, c=1 - c).wait_recv()
+        has_last = block_z(last) // 2 == own_q
+
+        @pl.when(jnp.logical_not(has_last))
+        def _():
+            drain_in(14, o_sem)
+
+        @pl.when(has_last)
+        def _():
+            drain_in(7, o_sem)
+            drain_in(7, last_sem.at[0])
+            drain_in(8, last_sem.at[1])
 
 
 def lay_out(parts, out, held, laid, in_sem, out_sem):
     rows = laid.shape[2]
     half = rows // 2
-    loads, stores = [], []
+    stores = []
+    def split(i):
+        mine = (lax.axis_index("yl") * 2 + lax.axis_index("c")) * 2 + i // 2
+        return mine == lax.rem(lax.axis_index("z") + 4, 8)
+
+    def load(i, side):
+        at = i // 2 * 16 + side * 8 + i % 2 * 4
+        return pltpu.make_async_copy(parts.at[pl.ds(at, 4)], held.at[i, side], in_sem.at[i, side])
+
     for i in range(4):
-        column, low = i // 2, i % 2 * 4
-        for side in range(2):
-            loads.append(pltpu.make_async_copy(
-                parts.at[column, pl.ds(side * 8 + low, 4)], held.at[i, side], in_sem.at[i, side]))
-            loads[-1].start()
-        stores.append(pltpu.make_async_copy(
-            laid.at[i], out.at[:, :, pl.ds(i * 4 * rows, 4 * rows)], out_sem.at[i]))
-    for i in range(4):
-        with scope("held"):
-            loads[2 * i].wait()
-            loads[2 * i + 1].wait()
+        load(i, 0).start()
+
+        @pl.when(split(i))
+        def _():
+            load(i, 1).start()
+
+        stores.append(pltpu.make_async_copy(laid.at[i], out.at[:, :, pl.ds(i * 4 * rows, 4 * rows)], out_sem.at[i]))
+
+    def place(i, both):
         for b in range(4):
-            block = held[i, 0, b].astype(F32) + held[i, 1, b].astype(F32)
+            block = held[i, 0, b].astype(F32)
+            if both:
+                block = block + held[i, 1, b].astype(F32)
             for part in range(2):
                 for side in range(2):
                     at = (side * 2 + part) * rows
                     laid[i, part, side * half:side * half + half, b * rows:b * rows + rows] = block[:, at:at + rows]
+
+    for i in range(4):
+        load(i, 0).wait()
+
+        @pl.when(split(i))
+        def _():
+            load(i, 1).wait()
+            place(i, True)
+
+        @pl.when(jnp.logical_not(split(i)))
+        def _():
+            place(i, False)
+
         stores[i].start()
-    with scope("stored"):
-        for store in stores:
+    for store in stores:
             store.wait()
 
 
@@ -398,7 +458,7 @@
     dma = pltpu.SemaphoreType.DMA
     parts = pl.pallas_call(
         kernel,
-        out_shape=jax.ShapeDtypeStruct((2, 16, half, 4 * slots), BF16),
+        out_shape=jax.ShapeDtypeStruct((32, half, 4 * slots), BF16),
         in_specs=[anywhere] * 6,
         out_specs=anywhere,
         scratch_shapes=[
@@ -411,16 +471,19 @@
             pltpu.VMEM((2, 8, half, 4 * slots), F32),
             pltpu.VMEM((8, 8, half, 4 * slots), BF16),
             pltpu.VMEM((8, 8, half, 4 * slots), BF16),
-            pltpu.VMEM((8, 8, half, 4 * slots), BF16),
+            pltpu.VMEM((8, 4, half, 4 * slots), BF16),
+            pltpu.VMEM((8, 4, half, 4 * slots), BF16),
+            pltpu.VMEM((2, 4, half, 4 * slots), F32),
+            pltpu.VMEM((32, half, 4 * slots), BF16),
+            pltpu.VMEM((8, half, 4 * slots), BF16),
             pltpu.VMEM((2, 16, slots, 128), F32),
             pltpu.VMEM((2, 8, 8, 2 * slots), F32),
             pltpu.VMEM((48, 128), F32),
             pltpu.VMEM((48, 128), jnp.int32),
             pltpu.VMEM((4, 16, 128), jnp.int32),
             pltpu.SMEM((2,), F32), pltpu.SMEM((2,), F32),
-            dma((10,)), dma((8,)), dma((5,)), dma((5,)), dma, dma,
-            dma((2, 2, 2)), dma((2, 2, 2)), dma((2, 4, 2)), dma((2, 4, 2)),
-            dma((8,)), dma((8,)), dma((8, 8)), dma((2, 16)),
+            dma((10,)), dma, dma((5,)), dma, dma, dma((2, 2, 2)), dma, dma((2, 4, 2)),
+            dma, dma((8,)), dma, dma((8,)), dma, dma, dma, dma, dma((2,)),
         ],
         compiler_params=pltpu.CompilerParams(
             collective_id=0, has_side_effects=True, vmem_limit_bytes=60 * 1024 * 1024),

time: 61.3 us -> 59.9 us (0.977)
  the two profiles are of different devices: /device:TPU:73 before, /device:TPU:1 now
where the time goes in v4:
time: 59.9 us; the launch traced here: 59.5 us
  Pallas kernels  59.5 us (99%)
    pallas_call x1, Pallas kernels, on_device(): pl.pallas_call(kernel, out_shape=jax.ShapeDtypeStruct((32, half, 4 * slot...  57.3 us
    pallas_call x1, Pallas kernels, on_device(): pl.pallas_call(lay_out, out_shape=jax.ShapeDtypeStruct((2, slots, 16 * sl...  2.25 us

profile of v4, /device:TPU:1, one launch (start us, length us, event | category | flops | bytes accessed | tf_op | source)
XLA Modules:
  0.0 59.5 jit_solution(5458417946835529218)
XLA Ops:
  0.0 57.3 %self_energy.1.parts = bf16[32,48,384]{2,1,0:T(8,128)(2,1)} custom-call(bf16[2,96,512]{2,1,0:T(8,128)(2,1)} %elements.1, bf16[2,2,512,2048]{3,2,1,0:T(8,128)(2,1)} %screened.1, f32[48,128]{1,0:T(8,128)} %bitcast.2, s32[48,128]{1,0:T(8,128)} %bitcast.3, f32[2]{0:T(128)} %points.1, f32[2]{0:T(128)} %weights.1), custom_call_target="tpu_custom_call" | custom-call | tf_op jit(solution)/shard_map/self_energy/pallas_call | solution.py:459
  57.3 2.2 %lay_out.1 = f32[2,96,1536]{2,1,0:T(8,128)} custom-call(bf16[32,48,384]{2,1,0:T(8,128)(2,1)} %self_energy.1.parts), custom_call_target="tpu_custom_call" | custom-call | tf_op jit(solution)/shard_map/lay_out/pallas_call | solution.py:492

commit v5 on v4

--- a/solution.py
+++ b/solution.py
@@ -19,9 +19,9 @@
 
 def kernel(
     elements, screened, energies, bands, points, weights, o_recv,
-    e_full, e_plane, w_buf, acc, y_buf, y_swap, s_sum, x_send, x_recv, h_send, h_recv, h_keep, o_buf, last_buf, s_col, s_row,
+    e_full, e_ring, e_plane, w_buf, acc, acc_near, y_buf, y_swap, s_sum, x_send, x_recv, h_send, h_recv, h_keep, o_buf, last_buf, s_col, s_row,
     energy_buf, band_buf, band_table, point_buf, weight_buf,
-    load_sem, p_send, p_recv, a_recv, xr_send, xr_recv, z_send, z_recv,
+    load_sem, p_send, p_recv, a_recv, xr_send, xr_recv, er_send, er_recv, share_recv, s_send, s_recv, z_send, z_recv,
     d_send, d_recv, hs_send, hs_recv, keep_sem, o_send, o_sem, last_send, last_sem,
 ):
     z, yh, x, yl, c = (lax.axis_index(name) for name in ("z", "yh", "x", "yl", "c"))
@@ -92,80 +92,38 @@
             ref = e_plane.at[way, block_at(k, behind)]
         return remote(ref, ref, xr_send, xr_recv.at[k, way, hop - 1], x=ahead)
 
+    def piece_of(ref, piece):
+        if piece == 0:
+            return ref.at[own_q]
+        return ref.at[quarter[2], :, :, pl.ds((piece - 1) * 256, 256)]
+
+    def ring(way, hop, piece):
+        src = piece_of(e_full if hop == 1 else e_ring.at[way], piece)
+        dst = piece_of(e_ring.at[way + 2 * hop - 2], piece)
+        return remote(src, dst, er_send, er_recv.at[way, hop - 1, piece], z=z_up if way == 0 else z_down)
+
+    def share(slot, piece):
+        ref = piece_of(e_ring.at[slot], piece)
+        return remote(ref, ref, er_send, share_recv.at[slot, piece], c=1 - c)
+
+    def ring_start(piece):
+        for way in range(2):
+            ring(way, 1, piece).start()
+
+    def ring_pass(hop, piece):
+        for way in range(2):
+            ring(way, hop, piece).wait_recv()
+            if hop == 1:
+                ring(way, 2, piece).start()
+            share(way + 2 * hop - 2, piece).start()
+
+    def shared(hop, piece):
+        for way in range(2):
+            share(way + 2 * hop - 2, piece).wait_recv()
+
+    ring_start(0)
     for way in range(2):
         x_copy(0, way, 1).start()
-
-    def terms(k, w, part, low, size):
-        lhs = e_full[quarter[k], :, :, low:low + size].reshape(2 * slots, size)
-        return dot_t(lhs, w_buf[k, w, part, :, low:low + size])
-
-    def accumulate(k, low=0, size=512):
-        for i in range(4):
-            term = terms(k, i // 2, i % 2, low, size)
-            acc[i] = term if k == 0 else acc[i] + term
-
-    with scope("quarter0"):
-        load_w[0].wait()
-        accumulate(0)
-
-    with scope("quarter1"):
-        to_c.wait_recv()
-        load_w[1].wait()
-        accumulate(1)
-
-    def pass_c(h):
-        ref = e_full.at[quarter[2], :, :, pl.ds(h * 256, 256)]
-        return remote(ref, ref, p_send, p_recv.at[2 * h + 1], c=1 - c)
-
-    other = e_full.at[quarter[2]]
-    to_a = remote(other, e_plane.at[:, own_b], p_send, a_recv, yh=1 - yh, yl=1 - yl)
-    load_w[2].wait()
-    load_w[3].wait()
-    with scope("wait_y0"):
-        to_y(0).wait_recv()
-    pass_c(0).start()
-    with scope("quarter2"):
-        accumulate(2, 0, 256)
-    with scope("wait_y1"):
-        to_y(1).wait_recv()
-    pass_c(1).start()
-    to_a.start()
-    with scope("quarter3"):
-        accumulate(2, 256, 256)
-        pass_c(0).wait_recv()
-        accumulate(3, 0, 256)
-    with scope("wait_c"):
-        pass_c(1).wait_recv()
-
-    def z_copy(way, hop, w):
-        ahead = z_up if way == 0 else z_down
-        owner = lax.rem(z + 8 - (hop - 1), 8) if way == 0 else lax.rem(z + hop - 1, 8)
-        ref = y_buf.at[w, owner]
-        return remote(ref, ref, z_send, z_recv.at[way, hop - 1, w], z=ahead)
-
-    with scope("applied"):
-        for w in range(2):
-            real = acc[2 * w] + terms(3, w, 0, 256, 256)
-            imag = acc[2 * w + 1] + terms(3, w, 1, 256, 256)
-            y_buf[w, z, 0] = (real[:slots] - imag[slots:]).astype(BF16)
-            y_buf[w, z, 1] = (imag[:slots] + real[slots:]).astype(BF16)
-            if w == 0:
-                z_copy(0, 1, 0).start()
-        z_copy(1, 1, 1).start()
-        z_copy(0, 1, 1).start()
-        z_copy(1, 1, 0).start()
-
-    def z_pass(hop, turn):
-        for way in range(2):
-            w = turn if way == 0 else 1 - turn
-            z_copy(way, hop, w).wait_recv()
-            if hop < 3 or (hop == 3 and turn == 0):
-                z_copy(way, hop + 1, w).start()
-
-    def x_pass(k):
-        for way in range(2):
-            x_copy(k, way, 1).wait_recv()
-            x_copy(k, way, 2).start()
 
     def spread_bands():
         rows = [band_buf[pl.ds(k, 16, stride=3), :] for k in range(3)]
@@ -175,6 +133,7 @@
         band_table[3] = jnp.concatenate([rows[2][:, 32:], rows[2][:, :32]], axis=1)
 
     def look_up(i, carry):
+        i = i + c * 8
         at = jnp.where(i < 8, z * 8 + i, (i - 8) * 8 + own_b)
         band = band_table[lax.rem(at, 4), pl.ds(at // 4, 1), :]
         band = jnp.broadcast_to(band, (128, 128)).T[:slots]
@@ -200,29 +159,158 @@
         s_row[w, g] = jnp.concatenate([one, one], axis=0).T[0:8]
         return carry
 
+    def look_up_some(n, m):
+        with scope("look_up"):
+            lax.fori_loop(n, m, look_up, 0)
+
+    def terms(k, w, part, low, size):
+        lhs = e_full[quarter[k], :, :, low:low + size].reshape(2 * slots, size)
+        return dot_t(lhs, w_buf[k, w, part, :, low:low + size])
+
+    def accumulate(k, low=0, size=512):
+        for i in range(4):
+            term = terms(k, i // 2, i % 2, low, size)
+            acc[i] = term if k == 0 else acc[i] + term
+
+    with scope("quarter0"):
+        load_w[0].wait()
+        accumulate(0)
+
+    with scope("quarter1"):
+        to_c.wait_recv()
+        load_w[1].wait()
+        accumulate(1)
+
+    def pass_c(h):
+        ref = e_full.at[quarter[2], :, :, pl.ds(h * 256, 256)]
+        return remote(ref, ref, p_send, p_recv.at[2 * h + 1], c=1 - c)
+
+    other = e_full.at[quarter[2]]
+    to_a = remote(other, e_plane.at[:, own_b], p_send, a_recv, yh=1 - yh, yl=1 - yl)
+    load_w[2].wait()
+    load_w[3].wait()
+    for load in load_s:
+        load.wait()
+    spread_bands()
+    look_up_some(0, 3)
+    with scope("wait_y0"):
+        to_y(0).wait_recv()
+    pass_c(0).start()
+    ring_start(1)
+    with scope("quarter2"):
+        accumulate(2, 0, 256)
+    look_up_some(3, 5)
+    with scope("quarter2b"):
+        pass_c(0).wait_recv()
+        accumulate(3, 0, 256)
+    with scope("wait_y1"):
+        to_y(1).wait_recv()
+    pass_c(1).start()
+    ring_start(2)
+    to_a.start()
+    with scope("quarter3"):
+        accumulate(2, 256, 256)
+    with scope("ring10"):
+        ring_pass(1, 0)
+    with scope("wait_c"):
+        pass_c(1).wait_recv()
+
+    def z_copy(way, hop, w):
+        ahead = z_up if way == 0 else z_down
+        owner = lax.rem(z + 8 - (hop - 1), 8) if way == 0 else lax.rem(z + hop - 1, 8)
+        ref = y_buf.at[w, owner]
+        return remote(ref, ref, z_send, z_recv.at[way, hop - 3, w], z=ahead)
+
+    def z_pass(hop, turn):
+        for way in range(2):
+            w = turn if way == 0 else 1 - turn
+            z_copy(way, hop, w).wait_recv()
+            if hop == 3 and turn == 0:
+                z_copy(way, 4, w).start()
+
+    def apply_to(w, zz, real, imag, low):
+        y_buf[w, zz, 0] = (real[low:low + slots] - imag[low + slots:low + 2 * slots]).astype(BF16)
+        y_buf[w, zz, 1] = (imag[low:low + slots] + real[low + slots:low + 2 * slots]).astype(BF16)
+
+    with scope("applied"):
+        for w in range(2):
+            apply_to(w, z, acc[2 * w] + terms(3, w, 0, 256, 256), acc[2 * w + 1] + terms(3, w, 1, 256, 256), 0)
+
+    def near_terms(hop, k, i):
+        lhs = e_ring[2 * hop - 2:2 * hop, quarter[k]].reshape(4 * slots, 512)
+        return dot_t(lhs, w_buf[k, i // 2, i % 2])
+
+    @scope("near")
+    def near(hop, k):
+        for i in range(4):
+            term = near_terms(hop, k, i)
+            acc_near[i] = term if k == 0 else acc_near[i] + term
+
+    @scope("near_applied")
+    def near_applied(hop, w):
+        real = acc_near[2 * w] + near_terms(hop, 3, 2 * w)
+        imag = acc_near[2 * w + 1] + near_terms(hop, 3, 2 * w + 1)
+        apply_to(w, lax.rem(z + 8 - hop, 8), real, imag, 0)
+        apply_to(w, lax.rem(z + hop, 8), real, imag, 2 * slots)
+
+    def x_pass(k):
+        for way in range(2):
+            x_copy(k, way, 1).wait_recv()
+            x_copy(k, way, 2).start()
+
+    def s_copy():
+        ref = s_col.at[:, pl.ds(c * 8, 8)]
+        return remote(ref, ref, s_send, s_recv, c=1 - c)
+
     with scope("x_pass0"):
         x_pass(0)
-    with scope("look_up0"):
-        for load in load_s:
-            load.wait()
-        spread_bands()
-        lax.fori_loop(0, 8, look_up, 0)
+    look_up_some(5, 6)
+    with scope("ring11"):
+        ring_pass(1, 1)
+    near(1, 0)
+    with scope("shared10"):
+        shared(1, 0)
+    near(1, 1)
+    with scope("ring12"):
+        ring_pass(1, 2)
+    look_up_some(6, 7)
+    near(1, 2)
     with scope("wait_a"):
         remote(other, e_plane.at[:, own_b], p_send, a_recv, yh=1 - yh, yl=1 - yl).wait_recv()
     for way in range(2):
         x_copy(1, way, 1).start()
-    with scope("z10"):
-        z_pass(1, 0)
-    with scope("look_up1"):
-        lax.fori_loop(8, 16, look_up, 0)
+    with scope("shared11"):
+        shared(1, 1)
+        shared(1, 2)
+    near_applied(1, 0)
+    near_applied(1, 1)
+    look_up_some(7, 8)
+    s_copy().start()
+    with scope("ring20"):
+        ring_pass(2, 0)
+    near(2, 0)
+    with scope("ring21"):
+        ring_pass(2, 1)
+    with scope("shared20"):
+        shared(2, 0)
+    near(2, 1)
     with scope("x_pass1"):
         x_pass(1)
-    with scope("z11"):
-        z_pass(1, 1)
+    with scope("ring22"):
+        ring_pass(2, 2)
+    near(2, 2)
+    with scope("shared21"):
+        shared(2, 1)
+        shared(2, 2)
+    near_applied(2, 0)
+    z_copy(0, 3, 0).start()
+    near_applied(2, 1)
+    z_copy(1, 3, 1).start()
+    z_copy(0, 3, 1).start()
+    z_copy(1, 3, 0).start()
     with scope("turn"):
+        s_copy().wait_recv()
         lax.fori_loop(0, 16, turn, 0)
-    with scope("z20"):
-        z_pass(2, 0)
     with scope("wait_x"):
         for k in range(2):
             for way in range(2):
@@ -281,7 +369,7 @@
             there = 4 - here
             h_send[t] = (s_sum[t % 2, pl.ds(there, 4)] + x_recv[t, pl.ds(there, 4)].astype(F32)).astype(BF16)
             partner(t).start()
-            h_keep[t % 2] = s_sum[t % 2, pl.ds(here, 4)] + x_recv[t, pl.ds(here, 4)].astype(F32)
+            h_keep[t] = s_sum[t % 2, pl.ds(here, 4)] + x_recv[t, pl.ds(here, 4)].astype(F32)
 
     def out_copy(t, dx):
         to_x = lax.rem(x + dx, 4)
@@ -296,7 +384,7 @@
         @pl.when(mine(t))
         def _():
             partner(t).wait_recv()
-            o_buf[t * 4:t * 4 + 4] = (h_keep[t % 2] + h_recv[t].astype(F32)).astype(BF16)
+            o_buf[t * 4:t * 4 + 4] = (h_keep[t] + h_recv[t].astype(F32)).astype(BF16)
             for dx in (2, 1, 3):
                 out_copy(t, dx).start()
 
@@ -335,20 +423,18 @@
     products(0)
     products(1)
     reduce(0)
+    products(2)
     reduce(1)
-    with scope("z21"):
-        z_pass(2, 1)
-    products(2)
-    complete(0)
-    complete(1)
+    products(3)
     reduce(2)
     with scope("z30"):
         z_pass(3, 0)
-    products(3)
     products(4)
+    reduce(3)
+    complete(0)
+    complete(1)
+    reduce(4)
     complete(2)
-    reduce(3)
-    reduce(4)
     with scope("z31"):
         z_pass(3, 1)
     products(5)
@@ -370,7 +456,9 @@
     with scope("wait_out"):
         drain(e_full, p_send)
         drain(e_plane.at[:, 0:6], xr_send)
-        drain(y_buf.at[:, 0:7], z_send)
+        drain(e_ring, er_send)
+        s_copy().wait_send()
+        drain(y_buf.at[:, 0:3], z_send)
         drain(x_send.at[0:4], d_send)
         keep(o_buf.at[0], 0).wait()
         keep(o_buf.at[0], 0).wait()
@@ -463,9 +551,11 @@
         out_specs=anywhere,
         scratch_shapes=[
             pltpu.VMEM((4, 2, slots, 512), BF16),
+            pltpu.VMEM((4, 4, 2, slots, 512), BF16),
             pltpu.VMEM((2, 8, slots, 512), BF16),
             pltpu.VMEM((4, 2, 2, 512, 512), BF16),
             pltpu.VMEM((4, 2 * slots, 512), F32),
+            pltpu.VMEM((4, 4 * slots, 512), F32),
             pltpu.VMEM((2, 8, 2, slots, 512), BF16),
             pltpu.VMEM((2, 2, slots, 512), BF16),
             pltpu.VMEM((2, 8, half, 4 * slots), F32),
@@ -473,7 +563,7 @@
             pltpu.VMEM((8, 8, half, 4 * slots), BF16),
             pltpu.VMEM((8, 4, half, 4 * slots), BF16),
             pltpu.VMEM((8, 4, half, 4 * slots), BF16),
-            pltpu.VMEM((2, 4, half, 4 * slots), F32),
+            pltpu.VMEM((8, 4, half, 4 * slots), F32),
             pltpu.VMEM((32, half, 4 * slots), BF16),
             pltpu.VMEM((8, half, 4 * slots), BF16),
             pltpu.VMEM((2, 16, slots, 128), F32),
@@ -482,7 +572,8 @@
             pltpu.VMEM((48, 128), jnp.int32),
             pltpu.VMEM((4, 16, 128), jnp.int32),
             pltpu.SMEM((2,), F32), pltpu.SMEM((2,), F32),
-            dma((10,)), dma, dma((5,)), dma, dma, dma((2, 2, 2)), dma, dma((2, 4, 2)),
+            dma((10,)), dma, dma((5,)), dma, dma, dma((2, 2, 2)),
+            dma, dma((2, 2, 3)), dma((4, 3)), dma, dma, dma, dma((2, 2, 2)),
             dma, dma((8,)), dma, dma((8,)), dma, dma, dma, dma, dma((2,)),
         ],
         compiler_params=pltpu.CompilerParams(

time: 59.9 us -> 58.8 us (0.982)
  Pallas kernels: 59.5 us -> 58.5 us
    pallas_call x1, Pallas kernels: 57.3 us -> 56.2 us  [on_device(): pl.pallas_call(kernel, out_shape=jax.ShapeDtypeStruct((32, half, 4 * slot...]
where the time goes in v5:
time: 58.8 us; the launch traced here: 58.7 us
  Pallas kernels  58.5 us (99%)
    pallas_call x1, Pallas kernels, on_device(): pl.pallas_call(kernel, out_shape=jax.ShapeDtypeStruct((32, half, 4 * slot...  56.2 us
    pallas_call x1, Pallas kernels, on_device(): pl.pallas_call(lay_out, out_shape=jax.ShapeDtypeStruct((2, slots, 16 * sl...  2.25 us

profile of v5, /device:TPU:1, one launch (start us, length us, event | category | flops | bytes accessed | tf_op | source)
XLA Modules:
  0.0 58.7 jit_solution(2168975636054612183)
XLA Ops:
  0.0 56.2 %self_energy.1.parts = bf16[32,48,384]{2,1,0:T(8,128)(2,1)} custom-call(bf16[2,96,512]{2,1,0:T(8,128)(2,1)} %elements.1, bf16[2,2,512,2048]{3,2,1,0:T(8,128)(2,1)} %screened.1, f32[48,128]{1,0:T(8,128)} %bitcast.2, s32[48,128]{1,0:T(8,128)} %bitcast.3, f32[2]{0:T(128)} %points.1, f32[2]{0:T(128)} %weights.1), custom_call_target="tpu_custom_call" | custom-call | tf_op jit(solution)/shard_map/self_energy/pallas_call | solution.py:547
  56.3 2.2 %lay_out.1 = f32[2,96,1536]{2,1,0:T(8,128)} custom-call(bf16[32,48,384]{2,1,0:T(8,128)(2,1)} %self_energy.1.parts), custom_call_target="tpu_custom_call" | custom-call | tf_op jit(solution)/shard_map/lay_out/pallas_call | solution.py:583

commit v6 on v5

--- a/solution.py
+++ b/solution.py
@@ -97,29 +97,26 @@
             return ref.at[own_q]
         return ref.at[quarter[2], :, :, pl.ds((piece - 1) * 256, 256)]
 
-    def ring(way, hop, piece):
-        src = piece_of(e_full if hop == 1 else e_ring.at[way], piece)
-        dst = piece_of(e_ring.at[way + 2 * hop - 2], piece)
-        return remote(src, dst, er_send, er_recv.at[way, hop - 1, piece], z=z_up if way == 0 else z_down)
-
-    def share(slot, piece):
-        ref = piece_of(e_ring.at[slot], piece)
-        return remote(ref, ref, er_send, share_recv.at[slot, piece], c=1 - c)
+    def ring(way, piece):
+        return remote(piece_of(e_full, piece), piece_of(e_ring.at[way], piece), er_send, er_recv.at[way, piece],
+                      z=z_up if way == 0 else z_down)
+
+    def share(way, piece):
+        ref = piece_of(e_ring.at[way], piece)
+        return remote(ref, ref, er_send, share_recv.at[way, piece], c=1 - c)
 
     def ring_start(piece):
         for way in range(2):
-            ring(way, 1, piece).start()
-
-    def ring_pass(hop, piece):
+            ring(way, piece).start()
+
+    def ring_pass(piece):
         for way in range(2):
-            ring(way, hop, piece).wait_recv()
-            if hop == 1:
-                ring(way, 2, piece).start()
-            share(way + 2 * hop - 2, piece).start()
-
-    def shared(hop, piece):
+            ring(way, piece).wait_recv()
+            share(way, piece).start()
+
+    def shared(piece):
         for way in range(2):
-            share(way + 2 * hop - 2, piece).wait_recv()
+            share(way, piece).wait_recv()
 
     ring_start(0)
     for way in range(2):
@@ -186,7 +183,11 @@
         return remote(ref, ref, p_send, p_recv.at[2 * h + 1], c=1 - c)
 
     other = e_full.at[quarter[2]]
-    to_a = remote(other, e_plane.at[:, own_b], p_send, a_recv, yh=1 - yh, yl=1 - yl)
+
+    def to_a(h):
+        cols = pl.ds(h * 256, 256)
+        return remote(other.at[:, :, cols], e_plane.at[:, own_b, :, cols], p_send, a_recv.at[h], yh=1 - yh, yl=1 - yl)
+
     load_w[2].wait()
     load_w[3].wait()
     for load in load_s:
@@ -197,6 +198,7 @@
         to_y(0).wait_recv()
     pass_c(0).start()
     ring_start(1)
+    to_a(0).start()
     with scope("quarter2"):
         accumulate(2, 0, 256)
     look_up_some(3, 5)
@@ -207,51 +209,48 @@
         to_y(1).wait_recv()
     pass_c(1).start()
     ring_start(2)
-    to_a.start()
+    to_a(1).start()
     with scope("quarter3"):
         accumulate(2, 256, 256)
-    with scope("ring10"):
-        ring_pass(1, 0)
-    with scope("wait_c"):
-        pass_c(1).wait_recv()
 
     def z_copy(way, hop, w):
         ahead = z_up if way == 0 else z_down
         owner = lax.rem(z + 8 - (hop - 1), 8) if way == 0 else lax.rem(z + hop - 1, 8)
         ref = y_buf.at[w, owner]
-        return remote(ref, ref, z_send, z_recv.at[way, hop - 3, w], z=ahead)
+        return remote(ref, ref, z_send, z_recv.at[way, hop - 2, w], z=ahead)
 
     def z_pass(hop, turn):
         for way in range(2):
             w = turn if way == 0 else 1 - turn
             z_copy(way, hop, w).wait_recv()
-            if hop == 3 and turn == 0:
-                z_copy(way, 4, w).start()
+            if hop == 2 or (hop == 3 and turn == 0):
+                z_copy(way, hop + 1, w).start()
 
     def apply_to(w, zz, real, imag, low):
         y_buf[w, zz, 0] = (real[low:low + slots] - imag[low + slots:low + 2 * slots]).astype(BF16)
         y_buf[w, zz, 1] = (imag[low:low + slots] + real[low + slots:low + 2 * slots]).astype(BF16)
 
-    with scope("applied"):
+    @scope("applied")
+    def applied():
         for w in range(2):
             apply_to(w, z, acc[2 * w] + terms(3, w, 0, 256, 256), acc[2 * w + 1] + terms(3, w, 1, 256, 256), 0)
 
-    def near_terms(hop, k, i):
-        lhs = e_ring[2 * hop - 2:2 * hop, quarter[k]].reshape(4 * slots, 512)
-        return dot_t(lhs, w_buf[k, i // 2, i % 2])
+    def near_terms(k, i, low, size):
+        lhs = e_ring[:, quarter[k], :, :, low:low + size].reshape(4 * slots, size)
+        return dot_t(lhs, w_buf[k, i // 2, i % 2, :, low:low + size])
 
     @scope("near")
-    def near(hop, k):
+    def near(k, low=0, size=512):
         for i in range(4):
-            term = near_terms(hop, k, i)
+            term = near_terms(k, i, low, size)
             acc_near[i] = term if k == 0 else acc_near[i] + term
 
     @scope("near_applied")
-    def near_applied(hop, w):
-        real = acc_near[2 * w] + near_terms(hop, 3, 2 * w)
-        imag = acc_near[2 * w + 1] + near_terms(hop, 3, 2 * w + 1)
-        apply_to(w, lax.rem(z + 8 - hop, 8), real, imag, 0)
-        apply_to(w, lax.rem(z + hop, 8), real, imag, 2 * slots)
+    def near_applied(w):
+        real = acc_near[2 * w] + near_terms(3, 2 * w, 256, 256)
+        imag = acc_near[2 * w + 1] + near_terms(3, 2 * w + 1, 256, 256)
+        apply_to(w, z_down, real, imag, 0)
+        apply_to(w, z_up, real, imag, 2 * slots)
 
     def x_pass(k):
         for way in range(2):
@@ -262,55 +261,48 @@
         ref = s_col.at[:, pl.ds(c * 8, 8)]
         return remote(ref, ref, s_send, s_recv, c=1 - c)
 
+    with scope("ring0"):
+        ring_pass(0)
+    near(0)
     with scope("x_pass0"):
         x_pass(0)
-    look_up_some(5, 6)
-    with scope("ring11"):
-        ring_pass(1, 1)
-    near(1, 0)
-    with scope("shared10"):
-        shared(1, 0)
-    near(1, 1)
-    with scope("ring12"):
-        ring_pass(1, 2)
-    look_up_some(6, 7)
-    near(1, 2)
+    with scope("shared0"):
+        shared(0)
+    with scope("ring1"):
+        ring_pass(1)
+    near(1)
+    near(2, 0, 256)
+    with scope("shared1"):
+        shared(1)
+    near(3, 0, 256)
     with scope("wait_a"):
-        remote(other, e_plane.at[:, own_b], p_send, a_recv, yh=1 - yh, yl=1 - yl).wait_recv()
+        to_a(0).wait_recv()
+        to_a(1).wait_recv()
     for way in range(2):
         x_copy(1, way, 1).start()
-    with scope("shared11"):
-        shared(1, 1)
-        shared(1, 2)
-    near_applied(1, 0)
-    near_applied(1, 1)
-    look_up_some(7, 8)
+    with scope("ring2"):
+        ring_pass(2)
+    near(2, 256, 256)
+    with scope("wait_c"):
+        pass_c(1).wait_recv()
+    applied()
+    with scope("shared2"):
+        shared(2)
+    near_applied(0)
+    z_copy(0, 2, 0).start()
+    near_applied(1)
+    z_copy(1, 2, 1).start()
+    z_copy(0, 2, 1).start()
+    z_copy(1, 2, 0).start()
+    look_up_some(5, 8)
     s_copy().start()
-    with scope("ring20"):
-        ring_pass(2, 0)
-    near(2, 0)
-    with scope("ring21"):
-        ring_pass(2, 1)
-    with scope("shared20"):
-        shared(2, 0)
-    near(2, 1)
     with scope("x_pass1"):
         x_pass(1)
-    with scope("ring22"):
-        ring_pass(2, 2)
-    near(2, 2)
-    with scope("shared21"):
-        shared(2, 1)
-        shared(2, 2)
-    near_applied(2, 0)
-    z_copy(0, 3, 0).start()
-    near_applied(2, 1)
-    z_copy(1, 3, 1).start()
-    z_copy(0, 3, 1).start()
-    z_copy(1, 3, 0).start()
     with scope("turn"):
         s_copy().wait_recv()
         lax.fori_loop(0, 16, turn, 0)
+    with scope("z20"):
+        z_pass(2, 0)
     with scope("wait_x"):
         for k in range(2):
             for way in range(2):
@@ -422,26 +414,28 @@
 
     products(0)
     products(1)
+    with scope("z21"):
+        z_pass(2, 1)
     reduce(0)
     products(2)
     reduce(1)
     products(3)
     reduce(2)
-    with scope("z30"):
-        z_pass(3, 0)
     products(4)
     reduce(3)
     complete(0)
+    with scope("z30"):
+        z_pass(3, 0)
+    reduce(4)
     complete(1)
-    reduce(4)
     complete(2)
     with scope("z31"):
         z_pass(3, 1)
     products(5)
+    complete(3)
     products(6)
-    complete(3)
+    reduce(5)
     complete(4)
-    reduce(5)
     reduce(6)
     with scope("z40"):
         z_pass(4, 0)
@@ -458,7 +452,7 @@
         drain(e_plane.at[:, 0:6], xr_send)
         drain(e_ring, er_send)
         s_copy().wait_send()
-        drain(y_buf.at[:, 0:3], z_send)
+        drain(y_buf.at[:, 0:5], z_send)
         drain(x_send.at[0:4], d_send)
         keep(o_buf.at[0], 0).wait()
         keep(o_buf.at[0], 0).wait()
@@ -551,7 +545,7 @@
         out_specs=anywhere,
         scratch_shapes=[
             pltpu.VMEM((4, 2, slots, 512), BF16),
-            pltpu.VMEM((4, 4, 2, slots, 512), BF16),
+            pltpu.VMEM((2, 4, 2, slots, 512), BF16),
             pltpu.VMEM((2, 8, slots, 512), BF16),
             pltpu.VMEM((4, 2, 2, 512, 512), BF16),
             pltpu.VMEM((4, 2 * slots, 512), F32),
@@ -572,8 +566,8 @@
             pltpu.VMEM((48, 128), jnp.int32),
             pltpu.VMEM((4, 16, 128), jnp.int32),
             pltpu.SMEM((2,), F32), pltpu.SMEM((2,), F32),
-            dma((10,)), dma, dma((5,)), dma, dma, dma((2, 2, 2)),
-            dma, dma((2, 2, 3)), dma((4, 3)), dma, dma, dma, dma((2, 2, 2)),
+            dma((10,)), dma, dma((5,)), dma((2,)), dma, dma((2, 2, 2)),
+            dma, dma((2, 3)), dma((2, 3)), dma, dma, dma, dma((2, 3, 2)),
             dma, dma((8,)), dma, dma((8,)), dma, dma, dma, dma, dma((2,)),
         ],
         compiler_params=pltpu.CompilerParams(

time: 58.8 us -> 57.5 us (0.978)
  Pallas kernels: 58.5 us -> 57.4 us
    pallas_call x1, Pallas kernels: 56.2 us -> 55.1 us  [on_device(): pl.pallas_call(kernel, out_shape=jax.ShapeDtypeStruct((32, half, 4 * slot...]
where the time goes in v6:
time: 57.5 us; the launch traced here: 57.4 us
  Pallas kernels  57.4 us (100%)
    pallas_call x1, Pallas kernels, on_device(): pl.pallas_call(kernel, out_shape=jax.ShapeDtypeStruct((32, half, 4 * slot...  55.1 us
    pallas_call x1, Pallas kernels, on_device(): pl.pallas_call(lay_out, out_shape=jax.ShapeDtypeStruct((2, slots, 16 * sl...  2.25 us

profile of v6, /device:TPU:1, one launch (start us, length us, event | category | flops | bytes accessed | tf_op | source)
XLA Modules:
  0.0 57.4 jit_solution(6761263826847059595)
XLA Ops:
  0.0 55.1 %self_energy.1.parts = bf16[32,48,384]{2,1,0:T(8,128)(2,1)} custom-call(bf16[2,96,512]{2,1,0:T(8,128)(2,1)} %elements.1, bf16[2,2,512,2048]{3,2,1,0:T(8,128)(2,1)} %screened.1, f32[48,128]{1,0:T(8,128)} %bitcast.2, s32[48,128]{1,0:T(8,128)} %bitcast.3, f32[2]{0:T(128)} %points.1, f32[2]{0:T(128)} %weights.1), custom_call_target="tpu_custom_call" | custom-call | tf_op jit(solution)/shard_map/self_energy/pallas_call | solution.py:541
  55.1 2.2 %lay_out.1 = f32[2,96,1536]{2,1,0:T(8,128)} custom-call(bf16[32,48,384]{2,1,0:T(8,128)(2,1)} %self_energy.1.parts), custom_call_target="tpu_custom_call" | custom-call | tf_op jit(solution)/shard_map/lay_out/pallas_call | solution.py:577

commit v7 on v6

--- a/solution.py
+++ b/solution.py
@@ -22,7 +22,7 @@
     e_full, e_ring, e_plane, w_buf, acc, acc_near, y_buf, y_swap, s_sum, x_send, x_recv, h_send, h_recv, h_keep, o_buf, last_buf, s_col, s_row,
     energy_buf, band_buf, band_table, point_buf, weight_buf,
     load_sem, p_send, p_recv, a_recv, xr_send, xr_recv, er_send, er_recv, share_recv, s_send, s_recv, z_send, z_recv,
-    d_send, d_recv, hs_send, hs_recv, keep_sem, o_send, o_sem, last_send, last_sem,
+    d_send, d_recv, l_recv, hs_send, hs_recv, keep_sem, o_send, o_sem, last_send, last_sem,
 ):
     z, yh, x, yl, c = (lax.axis_index(name) for name in ("z", "yh", "x", "yl", "c"))
     own_q = yl * 2 + c
@@ -210,9 +210,6 @@
     pass_c(1).start()
     ring_start(2)
     to_a(1).start()
-    with scope("quarter3"):
-        accumulate(2, 256, 256)
-
     def z_copy(way, hop, w):
         ahead = z_up if way == 0 else z_down
         owner = lax.rem(z + 8 - (hop - 1), 8) if way == 0 else lax.rem(z + hop - 1, 8)
@@ -266,12 +263,17 @@
     near(0)
     with scope("x_pass0"):
         x_pass(0)
+    with scope("quarter3"):
+        accumulate(2, 256, 256)
     with scope("shared0"):
         shared(0)
+    near(1)
     with scope("ring1"):
         ring_pass(1)
-    near(1)
     near(2, 0, 256)
+    with scope("wait_c"):
+        pass_c(1).wait_recv()
+    applied()
     with scope("shared1"):
         shared(1)
     near(3, 0, 256)
@@ -283,9 +285,6 @@
     with scope("ring2"):
         ring_pass(2)
     near(2, 256, 256)
-    with scope("wait_c"):
-        pass_c(1).wait_recv()
-    applied()
     with scope("shared2"):
         shared(2)
     near_applied(0)
@@ -320,23 +319,41 @@
     def across(t):
         return remote(x_send.at[t], x_recv.at[t], d_send, d_recv.at[t], c=1 - c)
 
-    @scope("products")
-    def products(t):
-        zz = block_z(t)
-        for w in range(2):
+    def swap(zz, ws=(0, 1)):
+        for w in ws:
             y_swap[w, 0] = y_buf[w, zz, 1]
             y_swap[w, 1] = -y_buf[w, zz, 0]
+
+    def rows_by_block(zz, at, ws=(0, 1)):
+        real = e_plane[0, at].reshape(4 * slots, 512)
+        imag = e_plane[1, at].reshape(4 * slots, 512)
+        total = None
+        for w in ws:
+            both = dot_t(real, y_buf[w, zz].reshape(2 * slots, 512)) + dot_t(imag, y_swap[w].reshape(2 * slots, 512))
+            s = s_col[w, at].reshape(4 * slots, 128)
+            factor = 0.5 * (jnp.concatenate([s, s[:, :2 * slots - 128]], axis=1) + s_row[w, zz][0:1])
+            total = both * factor if total is None else total + both * factor
+        total = total.reshape(4, slots, 2 * slots)
+        return jnp.concatenate([total[:, :half], total[:, half:]], axis=2)
+
+    @scope("products_first")
+    def products_first(t, w):
+        zz = block_z(t)
+        swap(zz, (w,))
         for i in range(2):
-            real = e_plane[0, i * 4:i * 4 + 4].reshape(4 * slots, 512)
-            imag = e_plane[1, i * 4:i * 4 + 4].reshape(4 * slots, 512)
-            total = None
-            for w in range(2):
-                both = dot_t(real, y_buf[w, zz].reshape(2 * slots, 512)) + dot_t(imag, y_swap[w].reshape(2 * slots, 512))
-                s = s_col[w, i * 4:i * 4 + 4].reshape(4 * slots, 128)
-                factor = 0.5 * (jnp.concatenate([s, s[:, :2 * slots - 128]], axis=1) + s_row[w, zz][0:1])
-                total = both * factor if total is None else total + both * factor
-            total = total.reshape(4, slots, 2 * slots)
-            s_sum[t % 2, i * 4:i * 4 + 4] = jnp.concatenate([total[:, :half], total[:, half:]], axis=2)
+            at = pl.ds(i * 4, 4)
+            s_sum[t % 2, at] = rows_by_block(zz, at, (w,))
+
+    @scope("products")
+    def products(t, w=None):
+        zz = block_z(t)
+        swap(zz, (0, 1) if w is None else (w,))
+        for i in range(2):
+            at = pl.ds(i * 4, 4)
+            if w is None:
+                s_sum[t % 2, at] = rows_by_block(zz, at)
+            else:
+                s_sum[t % 2, at] += rows_by_block(zz, at, (w,))
 
         @pl.when(jnp.logical_not(mine(t)))
         def _():
@@ -396,20 +413,40 @@
         return remote(last_buf.at[to_yh * 4 + to_x], o_recv.at[index], last_send, last_sem.at[0 if same else 1],
                       yh=to_yh, x=to_x, yl=yl if same else 1 - yl)
 
+    def last_rows(p):
+        return pl.ds((yh if p else 1 - yh) * 4, 4)
+
+    def last_across(p):
+        at = last_rows(p)
+        return remote(x_send.at[last, at], x_recv.at[last, at], d_send, l_recv.at[p], c=1 - c)
+
+    @scope("last_products")
+    def last_products(p):
+        zz, at = block_z(last), last_rows(p)
+        if p == 0:
+            swap(zz)
+        s_sum[last % 2, at] = rows_by_block(zz, at)
+
+        @pl.when(jnp.logical_not(mine(last)))
+        def _():
+            x_send[last, at] = s_sum[last % 2, at].astype(BF16)
+            last_across(p).start()
+
     @scope("finish")
-    def finish():
+    def finish(p):
+        at = last_rows(p)
+
         @pl.when(mine(last))
         def _():
-            across(last).wait_recv()
-            last_buf[...] = (s_sum[last % 2] + x_recv[last].astype(F32)).astype(BF16)
+            last_across(p).wait_recv()
+            last_buf[at] = (s_sum[last % 2, at] + x_recv[last, at].astype(F32)).astype(BF16)
             for same in (True, False):
                 @pl.when(same_yl(last) == same)
                 def _():
                     for dx in (2, 1, 3, 0):
-                        for dyh in (1, 0):
-                            if dx or dyh or not same:
-                                last_copy(dyh, dx, same).start()
-                    if same:
+                        if dx or p == 0 or not same:
+                            last_copy(1 - p, dx, same).start()
+                    if same and p:
                         keep(last_buf.at[own_b], last).start()
 
     products(0)
@@ -427,21 +464,25 @@
     with scope("z30"):
         z_pass(3, 0)
     reduce(4)
+    products_first(5, 0)
     complete(1)
+    products_first(6, 1)
     complete(2)
     with scope("z31"):
         z_pass(3, 1)
-    products(5)
+    products(5, 1)
+    products(6, 0)
+    reduce(5)
     complete(3)
-    products(6)
-    reduce(5)
+    reduce(6)
     complete(4)
-    reduce(6)
     with scope("z40"):
         z_pass(4, 0)
-    products(7)
-    finish()
+    last_products(0)
+    last_products(1)
+    finish(0)
     complete(5)
+    finish(1)
     complete(6)
 
     def drain(ref, sem):
@@ -568,7 +609,7 @@
             pltpu.SMEM((2,), F32), pltpu.SMEM((2,), F32),
             dma((10,)), dma, dma((5,)), dma((2,)), dma, dma((2, 2, 2)),
             dma, dma((2, 3)), dma((2, 3)), dma, dma, dma, dma((2, 3, 2)),
-            dma, dma((8,)), dma, dma((8,)), dma, dma, dma, dma, dma((2,)),
+            dma, dma((7,)), dma((2,)), dma, dma((7,)), dma, dma, dma, dma, dma((2,)),
         ],
         compiler_params=pltpu.CompilerParams(
             collective_id=0, has_side_effects=True, vmem_limit_bytes=60 * 1024 * 1024),

time: 57.5 us -> 56.4 us (0.981)
  Pallas kernels: 57.4 us -> 56.3 us
    pallas_call x1, Pallas kernels: 55.1 us -> 54 us  [on_device(): pl.pallas_call(kernel, out_shape=jax.ShapeDtypeStruct((32, half, 4 * slot...]
where the time goes in v7:
time: 56.4 us; the launch traced here: 56.3 us
  Pallas kernels  56.3 us (100%)
    pallas_call x1, Pallas kernels, on_device(): pl.pallas_call(kernel, out_shape=jax.ShapeDtypeStruct((32, half, 4 * slot...  54 us
    pallas_call x1, Pallas kernels, on_device(): pl.pallas_call(lay_out, out_shape=jax.ShapeDtypeStruct((2, slots, 16 * sl...  2.25 us

profile of v7, /device:TPU:1, one launch (start us, length us, event | category | flops | bytes accessed | tf_op | source)
XLA Modules:
  0.0 56.3 jit_solution(9681589851825945930)
XLA Ops:
  0.0 54.0 %self_energy.1.parts = bf16[32,48,384]{2,1,0:T(8,128)(2,1)} custom-call(bf16[2,96,512]{2,1,0:T(8,128)(2,1)} %elements.1, bf16[2,2,512,2048]{3,2,1,0:T(8,128)(2,1)} %screened.1, f32[48,128]{1,0:T(8,128)} %bitcast.2, s32[48,128]{1,0:T(8,128)} %bitcast.3, f32[2]{0:T(128)} %points.1, f32[2]{0:T(128)} %weights.1), custom_call_target="tpu_custom_call" | custom-call | tf_op jit(solution)/shard_map/self_energy/pallas_call | solution.py:582
  54.0 2.2 %lay_out.1 = f32[2,96,1536]{2,1,0:T(8,128)} custom-call(bf16[32,48,384]{2,1,0:T(8,128)(2,1)} %self_energy.1.parts), custom_call_target="tpu_custom_call" | custom-call | tf_op jit(solution)/shard_map/lay_out/pallas_call | solution.py:618

commit v8 on v7

--- a/solution.py
+++ b/solution.py
@@ -394,7 +394,7 @@
         def _():
             partner(t).wait_recv()
             o_buf[t * 4:t * 4 + 4] = (h_keep[t] + h_recv[t].astype(F32)).astype(BF16)
-            for dx in (2, 1, 3):
+            for dx in (2, 3, 1):
                 out_copy(t, dx).start()
 
             @pl.when(same_yl(t))
@@ -443,7 +443,7 @@
             for same in (True, False):
                 @pl.when(same_yl(last) == same)
                 def _():
-                    for dx in (2, 1, 3, 0):
+                    for dx in (2, 3, 1, 0):
                         if dx or p == 0 or not same:
                             last_copy(1 - p, dx, same).start()
                     if same and p:

time: 56.4 us -> 56.4 us (level)
  no operation moved by 1% of the time
where the time goes in v8:
time: 56.4 us; the launch traced here: 56.3 us
  Pallas kernels  56.3 us (100%)
    pallas_call x1, Pallas kernels, on_device(): pl.pallas_call(kernel, out_shape=jax.ShapeDtypeStruct((32, half, 4 * slot...  54.1 us
    pallas_call x1, Pallas kernels, on_device(): pl.pallas_call(lay_out, out_shape=jax.ShapeDtypeStruct((2, slots, 16 * sl...  2.25 us

profile of v8, /device:TPU:1, one launch (start us, length us, event | category | flops | bytes accessed | tf_op | source)
XLA Modules:
  0.0 56.3 jit_solution(5278358675367682833)
XLA Ops:
  0.0 54.1 %self_energy.1.parts = bf16[32,48,384]{2,1,0:T(8,128)(2,1)} custom-call(bf16[2,96,512]{2,1,0:T(8,128)(2,1)} %elements.1, bf16[2,2,512,2048]{3,2,1,0:T(8,128)(2,1)} %screened.1, f32[48,128]{1,0:T(8,128)} %bitcast.2, s32[48,128]{1,0:T(8,128)} %bitcast.3, f32[2]{0:T(128)} %points.1, f32[2]{0:T(128)} %weights.1), custom_call_target="tpu_custom_call" | custom-call | tf_op jit(solution)/shard_map/self_energy/pallas_call | solution.py:582
  54.1 2.2 %lay_out.1 = f32[2,96,1536]{2,1,0:T(8,128)} custom-call(bf16[32,48,384]{2,1,0:T(8,128)(2,1)} %self_energy.1.parts), custom_call_target="tpu_custom_call" | custom-call | tf_op jit(solution)/shard_map/lay_out/pallas_call | solution.py:618

commit v9 on v8

--- a/solution.py
+++ b/solution.py
@@ -86,10 +86,11 @@
 
     def x_copy(k, way, hop):
         ahead, behind = (x_up, x_down) if way == 0 else (x_down, x_up)
+        cols = pl.ds(0, 512) if k == 0 else pl.ds((k - 1) * 256, 256)
         if hop == 1:
-            ref = e_plane.at[:, block_at(k, x)]
+            ref = e_plane.at[:, block_at(k, x), :, cols]
         else:
-            ref = e_plane.at[way, block_at(k, behind)]
+            ref = e_plane.at[way, block_at(k, behind), :, cols]
         return remote(ref, ref, xr_send, xr_recv.at[k, way, hop - 1], x=ahead)
 
     def piece_of(ref, piece):
@@ -271,6 +272,10 @@
     with scope("ring1"):
         ring_pass(1)
     near(2, 0, 256)
+    with scope("wait_a0"):
+        to_a(0).wait_recv()
+    for way in range(2):
+        x_copy(1, way, 1).start()
     with scope("wait_c"):
         pass_c(1).wait_recv()
     applied()
@@ -278,10 +283,9 @@
         shared(1)
     near(3, 0, 256)
     with scope("wait_a"):
-        to_a(0).wait_recv()
         to_a(1).wait_recv()
     for way in range(2):
-        x_copy(1, way, 1).start()
+        x_copy(2, way, 1).start()
     with scope("ring2"):
         ring_pass(2)
     near(2, 256, 256)
@@ -297,13 +301,14 @@
     s_copy().start()
     with scope("x_pass1"):
         x_pass(1)
+        x_pass(2)
     with scope("turn"):
         s_copy().wait_recv()
         lax.fori_loop(0, 16, turn, 0)
     with scope("z20"):
         z_pass(2, 0)
     with scope("wait_x"):
-        for k in range(2):
+        for k in range(3):
             for way in range(2):
                 x_copy(k, way, 2).wait_recv()
 
@@ -607,7 +612,7 @@
             pltpu.VMEM((48, 128), jnp.int32),
             pltpu.VMEM((4, 16, 128), jnp.int32),
             pltpu.SMEM((2,), F32), pltpu.SMEM((2,), F32),
-            dma((10,)), dma, dma((5,)), dma((2,)), dma, dma((2, 2, 2)),
+            dma((10,)), dma, dma((5,)), dma((2,)), dma, dma((3, 2, 2)),
             dma, dma((2, 3)), dma((2, 3)), dma, dma, dma, dma((2, 3, 2)),
             dma, dma((7,)), dma((2,)), dma, dma((7,)), dma, dma, dma, dma, dma((2,)),
         ],

time: 56.4 us -> 57.2 us (1.014)
  Pallas kernels: 56.3 us -> 57.1 us
    pallas_call x1, Pallas kernels: 54.1 us -> 54.8 us  [on_device(): pl.pallas_call(kernel, out_shape=jax.ShapeDtypeStruct((32, half, 4 * slot...]
where the time goes in v9:
time: 57.2 us; the launch traced here: 57.1 us
  Pallas kernels  57.1 us (100%)
    pallas_call x1, Pallas kernels, on_device(): pl.pallas_call(kernel, out_shape=jax.ShapeDtypeStruct((32, half, 4 * slot...  54.8 us
    pallas_call x1, Pallas kernels, on_device(): pl.pallas_call(lay_out, out_shape=jax.ShapeDtypeStruct((2, slots, 16 * sl...  2.25 us

profile of v9, /device:TPU:1, one launch (start us, length us, event | category | flops | bytes accessed | tf_op | source)
XLA Modules:
  0.0 57.1 jit_solution(14188700584013838451)
XLA Ops:
  0.0 54.8 %self_energy.1.parts = bf16[32,48,384]{2,1,0:T(8,128)(2,1)} custom-call(bf16[2,96,512]{2,1,0:T(8,128)(2,1)} %elements.1, bf16[2,2,512,2048]{3,2,1,0:T(8,128)(2,1)} %screened.1, f32[48,128]{1,0:T(8,128)} %bitcast.2, s32[48,128]{1,0:T(8,128)} %bitcast.3, f32[2]{0:T(128)} %points.1, f32[2]{0:T(128)} %weights.1), custom_call_target="tpu_custom_call" | custom-call | tf_op jit(solution)/shard_map/self_energy/pallas_call | solution.py:587
  54.9 2.2 %lay_out.1 = f32[2,96,1536]{2,1,0:T(8,128)} custom-call(bf16[32,48,384]{2,1,0:T(8,128)(2,1)} %self_energy.1.parts), custom_call_target="tpu_custom_call" | custom-call | tf_op jit(solution)/shard_map/lay_out/pallas_call | solution.py:623
